TPU v7x, 256 devices: a whole 4x4x8 slice. The times are simulated.
256 devices in a mesh: seq: 32 (over z_hi, y, core), wgt: 8 (over x, z_lo).
Axes of the slice: x: 4, y: 4, z: 8 (z_hi: 4, z_lo: 2; z = z_hi * 2 + z_lo), core: 2. Of those that a mesh axis runs over, the one named last changes fastest.
Arguments:
- hidden: bfloat16 [12288, 5376], P('seq', 'wgt'), may hold values from -6 to 6
- q_weight: bfloat16 [2, 5376, 2048], P(None, 'seq', 'wgt'), may hold values from -448 to 448, as said below
- k_weight: bfloat16 [2, 5376, 1024], P(None, 'seq', 'wgt'), may hold values from -448 to 448, as said below
- v_weight: bfloat16 [2, 5376, 1024], P(None, 'seq', 'wgt'), may hold values from -448 to 448, as said below
- o_weight: bfloat16 [2, 2048, 5376], P(None, 'seq', 'wgt'), may hold values from -448 to 448, as said below
- q_scale: int32 [2, 42, 16], P(None, None, 'wgt'), may hold values from 113 to 117
- k_scale: int32 [2, 42, 8], P(None, None, 'wgt'), may hold values from 113 to 117
- v_scale: int32 [2, 42, 8], P(None, None, 'wgt'), may hold values from 113 to 117
- o_scale: int32 [2, 16, 42], replicated, may hold values from 113 to 117
- in_gain: float32 [2, 5376], replicated, may hold values from 0.5 to 1.5
- post_gain: float32 [2, 5376], P(None, 'wgt'), may hold values from 0.5 to 1.5
- q_gain: float32 [2, 128], replicated, may hold values from 0.1 to 1.9
- k_gain: float32 [2, 128], replicated, may hold values from 0.1 to 1.9
- windows: int32 [2], replicated, may hold values from 512 to 1024, as said below
Outputs:
- state: bfloat16 [12288, 5376], P('seq', 'wgt')
Inputs may be any that keep to these rules, and one draw needn't show every extreme that they name: `q_weight`: every entry is a finite value of the e4m3 floating-point format: sign, 3 mantissa bits, exponents of that format. `k_weight`: every entry is a finite value of the e4m3 floating-point format. `v_weight`: every entry is a finite value of the e4m3 floating-point format. `o_weight`: every entry is a finite value of the e4m3 floating-point format. `windows`: one layer's window is exactly 1024.
All inputs are finite; a program needn't handle non-finite values.
Results may differ from a plain program's by a relative error of at most 0.0095.
Values may be sent and summed in bfloat16 or wider, within the bound.
A program may use at most 128 MiB of HBM per device.

v0:
```python
import jax
import jax.numpy as jnp
from jax import lax
from jax.sharding import Mesh
from jax.sharding import PartitionSpec as P

HD = 128
BLOCK = 128
WINDOW = 1024
LAYERS = 2
WGT = ("wgt_0", "wgt_1")


eps = 1e-06
query_scale = 168.0 ** (-0.5)
rope_base = 10000.0


def in_one_piece(arrays, axis, dim, along):
    ends, at = ([], 0)
    for a in arrays[:-1]:
        at += a.shape[along]
        ends.append(at)
    both = jnp.concatenate(arrays, axis=along)
    return tuple(jnp.split(lax.all_gather(both, axis, axis=dim, tiled=True), ends, axis=along))


def gather_axes(array, axes, dim):
    if not axes:
        return array
    nearer = lax.all_gather(array, axes[-1], axis=dim, tiled=True)
    return gather_axes(nearer, axes[:-1], dim)


def passed_along(array, axis, by):
    size = lax.axis_size(axis)
    pairs = [(i, i + by) for i in range(size) if 0 <= i + by < size]
    return lax.ppermute(array, axis, pairs)


def in_order(pieces, dim):
    pieces = jnp.moveaxis(pieces, 0, dim)
    dims = pieces.shape
    return pieces.reshape(*dims[:dim], dims[dim] * dims[dim + 1], *dims[dim + 2 :])


def sent_to_all(array, axis):
    copies = jnp.broadcast_to(array, (lax.axis_size(axis), *array.shape))
    return lax.all_to_all(copies, axis, split_axis=0, concat_axis=0, tiled=True)


def collect(array, axis, dim):
    return in_order(sent_to_all(array, axis), dim)


def of_everyone(array, axis):
    everything = sent_to_all(array, axis)
    return jnp.sum(everything, axis=0)


def rmsnorm(values, gain):
    return values * lax.rsqrt(jnp.mean(values * values, axis=-1, keepdims=True) + eps) * gain


def rotate(values, position):
    half = values.shape[-1] // 2
    inverse = rope_base ** (-jnp.arange(half, dtype=jnp.float32) * 2.0 / values.shape[-1])
    angles = position.astype(jnp.float32)[:, None] * inverse[None, :]
    cosine = jnp.cos(angles)[:, None, :]
    sine = jnp.sin(angles)[:, None, :]
    first = values[..., :half]
    second = values[..., half:]
    return jnp.concatenate(
        [first * cosine - second * sine, second * cosine + first * sine], axis=-1
    )


def expand_scales(scale_codes):
    factor = jnp.exp2(scale_codes.astype(jnp.float32) - 127.0)
    return jnp.repeat(jnp.repeat(factor, BLOCK, axis=0), BLOCK, axis=1).astype(jnp.bfloat16)


def per_device(
    hidden,
    q_weight,
    k_weight,
    v_weight,
    o_weight,
    q_scale,
    k_scale,
    v_scale,
    o_scale,
    in_gain,
    post_gain,
    q_gain,
    k_gain,
    windows,
):
    local_rows = hidden.shape[0]
    width_share = hidden.shape[1]
    model_width = in_gain.shape[1]
    seq_index = lax.axis_index("seq")
    column_offset = lax.axis_index(WGT) * width_share
    halo_count = -(-(WINDOW - 1) // local_rows)
    position = seq_index * local_rows + jnp.arange(local_rows, dtype=jnp.int32)
    key_position = (
        seq_index * local_rows
        - halo_count * local_rows
        + jnp.arange((halo_count + 1) * local_rows, dtype=jnp.int32)
    )
    gap = position[:, None] - key_position[None, :]
    columns = column_offset + jnp.arange(width_share, dtype=jnp.int32)
    pick = (
        (columns // BLOCK)[None, :] == jnp.arange(model_width // BLOCK, dtype=jnp.int32)[:, None]
    ).astype(jnp.float32)
    gathered = (
        *in_one_piece((q_weight, k_weight, v_weight), "seq", 1, 2),
        lax.all_gather(o_weight, "seq", axis=1, tiled=True),
    )
    state = hidden
    for layer_idx in range(LAYERS):
        outgoing = state
        arriving = gather_axes(outgoing, WGT, 1)
        normed = rmsnorm(arriving.astype(jnp.float32), in_gain[layer_idx]).astype(jnp.bfloat16)
        tables = (
            expand_scales(q_scale[layer_idx]),
            expand_scales(k_scale[layer_idx]),
            expand_scales(v_scale[layer_idx]),
        )
        o_factor = jnp.exp2(o_scale[layer_idx].astype(jnp.float32) - 127.0)
        o_columns = jnp.dot(o_factor, pick, precision=lax.Precision.HIGHEST)
        o_table = jnp.repeat(o_columns, BLOCK, axis=0).astype(jnp.bfloat16)
        queries = jnp.dot(
            normed, gathered[0][layer_idx] * tables[0], preferred_element_type=jnp.float32
        )
        key_part = jnp.dot(
            normed, gathered[1][layer_idx] * tables[1], preferred_element_type=jnp.float32
        )
        value_part = jnp.dot(
            normed, gathered[2][layer_idx] * tables[2], preferred_element_type=jnp.float32
        )
        queries = (
            rotate(rmsnorm(queries.reshape(local_rows, -1, HD), q_gain[layer_idx]), position)
            * query_scale
        ).astype(jnp.bfloat16)
        key_heads = rotate(
            rmsnorm(key_part.reshape(local_rows, -1, HD), k_gain[layer_idx]), position
        ).astype(jnp.bfloat16)
        key_flat = key_heads.reshape(local_rows, -1)
        value_flat = value_part.astype(jnp.bfloat16)
        earlier = []
        for distance in range(1, halo_count + 1):
            earlier.insert(0, passed_along((key_flat, value_flat), "seq", distance))
        kv_local = key_flat.shape[1] // HD
        groups = queries.shape[1] // kv_local
        all_keys = jnp.concatenate([item[0] for item in earlier] + [key_flat], axis=0).reshape(
            -1, kv_local, HD
        )
        all_values = jnp.concatenate([item[1] for item in earlier] + [value_flat], axis=0).reshape(
            -1, kv_local, HD
        )
        grouped = queries.reshape(local_rows, kv_local, groups, HD)
        scores = jnp.einsum("qkgd,skd->kgqs", grouped, all_keys, preferred_element_type=jnp.float32)
        allowed = (key_position[None, :] >= 0) & (gap >= 0) & (gap < windows[layer_idx])
        scores = jnp.where(allowed, scores, -1e30)
        top = jnp.max(scores, axis=-1, keepdims=True)
        expval = jnp.exp(scores - top)
        weights = (expval / jnp.sum(expval, axis=-1, keepdims=True)).astype(jnp.bfloat16)
        mixed = jnp.einsum(
            "kgqs,skd->qkgd", weights, all_values, preferred_element_type=jnp.float32
        )
        mixed = mixed.reshape(local_rows, -1).astype(jnp.bfloat16)
        mixed_full = collect(mixed, WGT, 1)
        projected = jnp.dot(
            mixed_full, gathered[3][layer_idx] * o_table, preferred_element_type=jnp.float32
        )
        post_squares = of_everyone(jnp.sum(projected * projected, axis=-1), WGT)
        post = (
            projected
            * lax.rsqrt(post_squares / model_width + eps)[:, None]
            * post_gain[layer_idx][None, :]
        )
        state = (state.astype(jnp.float32) + post).astype(jnp.bfloat16)
    return state


def solution(mesh):
    torus = Mesh(mesh.devices.reshape(mesh.shape["seq"], 4, 2), ("seq", "wgt_0", "wgt_1"))
    in_specs = (
        P("seq", WGT),
        P(None, "seq", WGT),
        P(None, "seq", WGT),
        P(None, "seq", WGT),
        P(None, "seq", WGT),
        P(None, None, WGT),
        P(None, None, WGT),
        P(None, None, WGT),
        P(),
        P(),
        P(None, WGT),
        P(),
        P(),
        P(),
    )
    out_specs = P("seq", WGT)
    return jax.shard_map(
        per_device, mesh=torus, in_specs=in_specs, out_specs=out_specs, check_vma=False
    )
```

profile of v0, /device:TPU:64, one launch (start us, length us, event | category | flops | bytes accessed | tf_op | source)
XLA Modules:
  0.0 430.0 jit_solution(10777370978775861728)
XLA Ops:
  6.5 16.4 %all_gather.18 = bf16[384,1344]{0,1:T(8,128)(2,1)} all-gather(bf16[384,672]{0,1:T(8,128)(2,1)} %param.14), channel_id=1, replica_groups=mesh['seq'=32,'wgt_0'=4,'wgt_1'=2] {'wgt_1'}, dimensions={1}, use_global_device_ids=true | all-gather | bytes 1548288 | tf_op jit(solution)/shard_map/all_gather | solution.py:31
  32.4 3.7 fusion.28
  36.0 38.6 %all-gather.5.cloned.1.call-done = bf16[384,5376]{0,1:T(8,128)(2,1)} async-done(((bf16[384,1344]{0,1:T(8,128)(2,1)}), bf16[384,5376]{0,1:T(8,128)(2,1)}) %all-gather.5.cloned.1.call-update) | async-done | bytes 4128784 | tf_op jit(solution)/shard_map/all_gather | solution.py:31
  77.8 85.7 %all-gather.7.cloned.1.call-done = bf16[2,5376,512]{2,1,0:T(8,128)(2,1)} async-done(((bf16[2,168,512]{2,1,0:T(8,128)(2,1)}), bf16[2,5376,512]{2,1,0:T(8,128)(2,1)}) %all-gather.7.cloned.1.call-update) | async-done | bytes 11010064 | tf_op jit(solution)/shard_map/all_gather | solution.py:25
  163.5 7.2 %multiply_reduce_fusion.5 = (f32[384]{0:T(512)S(1)}, f32[384,128]{0,1:T(8,128)S(1)}) fusion(bf16[2,5376,512]{2,1,0:T(8,128)(2,1)} %all-gather.7.cloned.1.call-done, bf16[5376]{0:T(1024)(128)(2,1)S(1)} %broadcast_bitcast_fusion.2, bf16[384,5376]{0,1:T(8,128)(2,1)} %all-gather.5.cloned.1.call-done, f32[5376]{0:T(1024)S(1)} %get-tuple-element.6, ...), kind=kOutput, calls=%fused_computation.124 | convolution fusion | flops 537525888 | bytes 5736960 | tf_op jit(solution)/shard_map/dot_general | solution.py:136
  171.9 8.5 %collective-permute-start.3 = (bf16[384,128]{0,1:T(8,128)(2,1)}, bf16[384,128]{0,1:T(8,128)(2,1)}, u32[]{:S(2)}, u32[]{:S(2)}) collective-permute-start(bf16[384,128]{0,1:T(8,128)(2,1)} %pad_maximum_fusion.1), channel_id=1, source_target_pairs={{0,24},{8,32},{16,40},{24,48},{32,56},{40,64},{48,72},{56,80},{64,... | collective-permute-start | bytes 294920 | tf_op jit(solution)/shard_map/ppermute | solution.py:38
  184.5 5.1 %fusion.47 = bf16[384,128]{1,0:T(8,128)(2,1)} fusion(bf16[2,5376,512]{2,1,0:T(8,128)(2,1)} %all-gather.7.cloned.1.call-done, bf16[5376]{0:T(1024)(128)(2,1)S(1)} %broadcast_bitcast_fusion.3, bf16[384,5376]{0,1:T(8,128)(2,1)S(1)} %copy-done, f32[5376]{0:T(1024)S(1)} %get-tuple-element.6, f32[384]{0:T(512)S(1)} %add_rsqrt_fusion.7), kind=kOutput, calls=%fused_computation.60 | convolution fusion | flops 537477120 | bytes 5637120 | tf_op jit(solution)/shard_map/dot_general | solution.py:139
  189.6 5.1 %collective-permute-start = (bf16[384,128]{1,0:T(8,128)(2,1)}, bf16[384,128]{1,0:T(8,128)(2,1)}, u32[]{:S(2)}, u32[]{:S(2)}) collective-permute-start(bf16[384,128]{1,0:T(8,128)(2,1)} %fusion.47), channel_id=1, source_target_pairs={{0,24},{8,32},{16,40},{24,48},{32,56},{40,64},{48,72},{56,80},{64,... | collective-permute-start | bytes 294920 | tf_op jit(solution)/shard_map/ppermute | solution.py:38
  194.7 3.9 collective-permute-start.1
  198.9 6.8 %broadcast_in_dim.44 = bf16[5376,2,128]{2,1,0:T(2,128)(2,1)S(1)} broadcast(bf16[5376,2]{1,0:T(8,128)(2,1)S(1)} %bitcast.206), dimensions={0,1} | broadcast | bytes 2774016 | tf_op jit(solution)/shard_map/broadcast_in_dim | solution.py:80
  205.9 6.8 %broadcast_in_dim.53 = bf16[5376,2,128]{2,1,0:T(2,128)(2,1)S(1)} broadcast(bf16[5376,2]{1,0:T(8,128)(2,1)S(1)} %bitcast.207), dimensions={0,1} | broadcast | bytes 2774016 | tf_op jit(solution)/shard_map/broadcast_in_dim | solution.py:80
  215.1 4.5 %copy.88 = bf16[256,5376]{1,0:T(8,128)(2,1)} copy(bf16[256,5376]{0,1:T(8,128)(2,1)} %get-tuple-element.10) | data formatting | bytes 5505024 | tf_op jit(solution)/shard_map/dot_general | solution.py:133
  219.6 5.0 %multiply_reduce_fusion.3 = (f32[384,2]{0,1:T(2,128)S(1)}, f32[384,2,128]{0,2,1:T(8,128)S(1)}) fusion(bf16[2,128,5376]{2,1,0:T(8,128)(2,1)} %bitcast.213, f32[5376]{0:T(1024)S(1)} %get-tuple-element.6, f32[384]{0:T(512)S(1)} %add_rsqrt_fusion.7, bf16[384,5376]{0,1:T(8,128)(2,1)} %all-gather.5.cloned.1.call-done), kind=kOutput, calls=%fused_computation.113 | convolution fusion | flops 1065417984 | bytes 7300608 | tf_op jit(solution)/shard_map/dot_general | solution.py:133
  230.5 11.4 %collective-permute-done.2 = bf16[384,128]{1,0:T(8,128)(2,1)S(1)} collective-permute-done((bf16[384,128]{1,0:T(8,128)(2,1)}, bf16[384,128]{1,0:T(8,128)(2,1)S(1)}, u32[]{:S(2)}, u32[]{:S(2)}) %collective-permute-start.2) | collective-permute-done | bytes 98336 | tf_op jit(solution)/shard_map/ppermute | solution.py:38
  245.6 4.3 all-to-all-start
  250.2 14.1 %all-to-all-done = bf16[8,384,256]{1,2,0:T(8,128)(2,1)} async-done(((bf16[8,384,256]{1,2,0:T(8,128)(2,1)}), bf16[8,384,256]{1,2,0:T(8,128)(2,1)}, u32[]{:S(2)}, u32[]{:S(2)}) %all-to-all-start) | async-done | bytes 1572896 | tf_op jit(solution)/shard_map/all_to_all | solution.py:49
  264.5 5.1 %multiply_reduce_fusion.1 = (f32[384]{0:T(512)S(1)}, f32[384,672]{0,1:T(8,128)}) fusion(bf16[384,2048]{0,1:T(8,128)(2,1)} %bitcast.27, bf16[1,2048,672]{2,1,0:T(8,128)(2,1)S(1)} %bitcast.209, bf16[2,2048,672]{2,1,0:T(8,128)(2,1)} %all-gather.9.cloned.1.call-done), kind=kOutput, calls=%fused_computation.67 | convolution fusion | flops 1058856576 | bytes 8504832 | tf_op jit(solution)/shard_map/dot_general | solution.py:174
  270.2 3.3 all-to-all-start.1
  273.7 6.0 %all-to-all-done.1 = f32[8,1,384]{2,1,0:T(1,128)S(1)} async-done(((f32[8,1,384]{2,1,0:T(1,128)}), f32[8,1,384]{2,1,0:T(1,128)S(1)}, u32[]{:S(2)}, u32[]{:S(2)}) %all-to-all-start.1) | async-done | bytes 12320 | tf_op jit(solution)/shard_map/all_to_all | solution.py:49
  281.3 10.1 %all_gather.22 = bf16[384,1344]{0,1:T(8,128)(2,1)} all-gather(bf16[384,672]{0,1:T(8,128)(2,1)S(1)} %add_convert_fusion.1), channel_id=1, replica_groups=mesh['seq'=32,'wgt_0'=4,'wgt_1'=2] {'wgt_1'}, dimensions={1}, use_global_device_ids=true | all-gather | bytes 1548288 | tf_op jit(solution)/shard_map/all_gather | solution.py:31
  294.5 46.1 %all-gather.11.cloned.1.call-done = bf16[384,5376]{0,1:T(8,128)(2,1)} async-done(((bf16[384,1344]{0,1:T(8,128)(2,1)}), bf16[384,5376]{0,1:T(8,128)(2,1)}) %all-gather.11.cloned.1.call-update) | async-done | bytes 4128784 | tf_op jit(solution)/shard_map/all_gather | solution.py:31
  340.6 3.3 fusion.3
  344.0 4.5 %fusion.50 = bf16[384,128]{1,0:T(8,128)(2,1)S(1)} fusion(bf16[2,5376,512]{2,1,0:T(8,128)(2,1)} %all-gather.7.cloned.1.call-done, bf16[5376]{0:T(1024)(128)(2,1)S(1)} %broadcast_bitcast_fusion.1, bf16[384,5376]{0,1:T(8,128)(2,1)S(1)} %copy-done.1, f32[5376]{0:T(1024)S(1)} %get-tuple-element.5, f32[384]{0:T(512)S(1)} %add_rsqrt_fusion.4), kind=kOutput, calls=%fused_computation.61 | convolution fusion | flops 537477120 | bytes 5637120 | tf_op jit(solution)/shard_map/dot_general | solution.py:139
  351.4 3.4 collective-permute-start.7
  354.8 4.1 multiply_reduce_fusion.4
  362.6 4.7 %collective-permute-start.11 = (bf16[384,128]{0,1:T(8,128)(2,1)S(1)}, bf16[384,128]{0,1:T(8,128)(2,1)S(1)}, u32[]{:S(2)}, u32[]{:S(2)}) collective-permute-start(bf16[384,128]{0,1:T(8,128)(2,1)S(1)} %pad_maximum_fusion.2), channel_id=1, source_target_pairs={{0,8},{8,16},{16,24},{24,32},{32,40},{40,48},{48,56},{56,64},{64,7... | collective-permute-start | bytes 294920 | tf_op jit(solution)/shard_map/ppermute | solution.py:38
  367.3 4.0 collective-permute-start.9
  373.3 4.4 %collective-permute-start.8 = (bf16[384,128]{1,0:T(8,128)(2,1)S(1)}, bf16[384,128]{1,0:T(8,128)(2,1)S(1)}, u32[]{:S(2)}, u32[]{:S(2)}) collective-permute-start(bf16[384,128]{1,0:T(8,128)(2,1)S(1)} %fusion.50), channel_id=1, source_target_pairs={{0,8},{8,16},{16,24},{24,32},{32,40},{40,48},{48,56},{56,64},{64,7... | collective-permute-start | bytes 294920 | tf_op jit(solution)/shard_map/ppermute | solution.py:38
  385.1 5.1 %all-to-all-start.2 = ((bf16[8,384,256]{1,2,0:T(8,128)(2,1)}), bf16[8,384,256]{1,2,0:T(8,128)(2,1)S(1)}, u32[]{:S(2)}, u32[]{:S(2)}) async-start(bf16[8,384,256]{1,2,0:T(8,128)(2,1)} %broadcast_in_dim.54), calls=%async_computation.2 | async-start | bytes 3145728 | tf_op jit(solution)/shard_map/all_to_all | solution.py:49
  390.4 19.3 %all-to-all-done.2 = bf16[8,384,256]{1,2,0:T(8,128)(2,1)S(1)} async-done(((bf16[8,384,256]{1,2,0:T(8,128)(2,1)}), bf16[8,384,256]{1,2,0:T(8,128)(2,1)S(1)}, u32[]{:S(2)}, u32[]{:S(2)}) %all-to-all-start.2) | async-done | bytes 1572896 | tf_op jit(solution)/shard_map/all_to_all | solution.py:49
  410.0 3.7 multiply_reduce_fusion
  413.7 8.7 %all_to_all.22 = f32[8,1,384]{2,1,0:T(1,128)S(1)} all-to-all(f32[8,1,384]{2,1,0:T(1,128)S(1)} %broadcast_in_dim.108), channel_id=1, replica_groups=mesh['seq'=32,'wgt_0'=4,'wgt_1'=2] {'wgt_0','wgt_1'}, dimensions={0} | all-to-all | bytes 24576 | tf_op jit(solution)/shard_map/all_to_all | solution.py:49
  (111 shorter events, 53.2 us)
Async XLA Ops:
  6.5 68.1 %all-gather.5.cloned.1.call-start = ((), (), s32[]{:S(2)}) async-start(), calls=%async_computation.4 | async-start | bytes 5160960 | tf_op jit(solution)/shard_map/all_gather | solution.py:31
  23.0 140.6 %all-gather.7.cloned.1.call-start = ((), (), s32[]{:S(2)}) async-start(), calls=%async_computation.5 | async-start | bytes 11354112 | tf_op jit(solution)/shard_map/all_gather | solution.py:25
  24.8 225.3 %all-gather.9.cloned.1.call-start = ((), (), s32[]{:S(2)}) async-start(), calls=%async_computation.6 | async-start | bytes 6488064 | tf_op jit(solution)/shard_map/all_gather | solution.py:118
  163.5 20.9 %copy-start = (bf16[384,5376]{0,1:T(8,128)(2,1)S(1)}, bf16[384,5376]{0,1:T(8,128)(2,1)}, u32[]{:S(2)}) copy-start(bf16[384,5376]{0,1:T(8,128)(2,1)} %all-gather.5.cloned.1.call-done) | copy-start | bytes 12386308
  171.9 52.9 %collective-permute-start.3 = (bf16[384,128]{0,1:T(8,128)(2,1)}, bf16[384,128]{0,1:T(8,128)(2,1)}, u32[]{:S(2)}, u32[]{:S(2)}) collective-permute-start(bf16[384,128]{0,1:T(8,128)(2,1)} %pad_maximum_fusion.1), channel_id=1, source_target_pairs={{0,24},{8,32},{16,40},{24,48},{32,56},{40,64},{48,72},{56,80},{64,... | collective-permute-start | bytes 294920 | tf_op jit(solution)/shard_map/ppermute | solution.py:38
  180.5 47.1 %collective-permute-start.4 = (bf16[384,128]{0,1:T(8,128)(2,1)}, bf16[384,128]{0,1:T(8,128)(2,1)}, u32[]{:S(2)}, u32[]{:S(2)}) collective-permute-start(bf16[384,128]{0,1:T(8,128)(2,1)} %pad_maximum_fusion.1), channel_id=1, source_target_pairs={{0,16},{8,24},{16,32},{24,40},{32,48},{40,56},{48,64},{56,72},{64,... | collective-permute-start | bytes 294920 | tf_op jit(solution)/shard_map/ppermute | solution.py:38
  182.5 45.0 %collective-permute-start.5 = (bf16[384,128]{0,1:T(8,128)(2,1)}, bf16[384,128]{0,1:T(8,128)(2,1)}, u32[]{:S(2)}, u32[]{:S(2)}) collective-permute-start(bf16[384,128]{0,1:T(8,128)(2,1)} %pad_maximum_fusion.1), channel_id=1, source_target_pairs={{0,8},{8,16},{16,24},{24,32},{32,40},{40,48},{48,56},{56,64},{64,7... | collective-permute-start | bytes 294920 | tf_op jit(solution)/shard_map/ppermute | solution.py:38
  184.5 28.2 %slice-start = ((s8[11010048]{0:T(1024)(128)(4,1)}), s8[4194304]{0:T(1024)(128)(4,1)S(1)}, s32[]{:S(2)}) async-start(s8[11010048]{0:T(1024)(128)(4,1)} %bitcast.210), calls=%async_computation.8 | async-start | bytes 8388608
  184.5 28.2 %slice-start.1 = ((s8[11010048]{0:T(1024)(128)(4,1)}), s8[4194304]{0:T(1024)(128)(4,1)S(1)}, s32[]{:S(2)}) async-start(s8[11010048]{0:T(1024)(128)(4,1)} %bitcast.210), calls=%async_computation.9 | async-start | bytes 8388608
  189.6 40.9 %collective-permute-start = (bf16[384,128]{1,0:T(8,128)(2,1)}, bf16[384,128]{1,0:T(8,128)(2,1)}, u32[]{:S(2)}, u32[]{:S(2)}) collective-permute-start(bf16[384,128]{1,0:T(8,128)(2,1)} %fusion.47), channel_id=1, source_target_pairs={{0,24},{8,32},{16,40},{24,48},{32,56},{40,64},{48,72},{56,80},{64,... | collective-permute-start | bytes 294920 | tf_op jit(solution)/shard_map/ppermute | solution.py:38
  194.7 35.8 %collective-permute-start.1 = (bf16[384,128]{1,0:T(8,128)(2,1)}, bf16[384,128]{1,0:T(8,128)(2,1)}, u32[]{:S(2)}, u32[]{:S(2)}) collective-permute-start(bf16[384,128]{1,0:T(8,128)(2,1)} %fusion.47), channel_id=1, source_target_pairs={{0,16},{8,24},{16,32},{24,40},{32,48},{40,56},{48,64},{56,72},{64,... | collective-permute-start | bytes 294920 | tf_op jit(solution)/shard_map/ppermute | solution.py:38
  198.9 13.8 %slice-start.2 = ((s8[11010048]{0:T(1024)(128)(4,1)}), s8[2621440]{0:T(1024)(128)(4,1)S(1)}, s32[]{:S(2)}) async-start(s8[11010048]{0:T(1024)(128)(4,1)} %bitcast.210), calls=%async_computation.10 | async-start | bytes 5242880
  219.6 8.0 %copy-start.4 = (pred[384,1536]{0,1:T(8,128)(4,1)S(1)}, pred[384,1536]{0,1:T(8,128)(4,1)}, u32[]{:S(2)}) copy-start(pred[384,1536]{0,1:T(8,128)(4,1)} %get-tuple-element.20) | copy-start | bytes 1769476
  224.8 17.1 %collective-permute-start.2 = (bf16[384,128]{1,0:T(8,128)(2,1)}, bf16[384,128]{1,0:T(8,128)(2,1)S(1)}, u32[]{:S(2)}, u32[]{:S(2)}) collective-permute-start(bf16[384,128]{1,0:T(8,128)(2,1)} %fusion.47), channel_id=1, source_target_pairs={{0,8},{8,16},{16,24},{24,32},{32,40},{40,48},{48,56},{56,64},{64,7... | collective-permute-start | bytes 294920 | tf_op jit(solution)/shard_map/ppermute | solution.py:38
  244.3 5.7 %copy-start.6 = (s32[2,16,42]{2,1,0:T(8,128)S(1)}, s32[2,16,42]{2,1,0:T(8,128)}, u32[]{:S(2)}) copy-start(s32[2,16,42]{2,1,0:T(8,128)} %param.22) | copy-start | bytes 16132
  245.6 18.7 %all-to-all-start = ((bf16[8,384,256]{1,2,0:T(8,128)(2,1)}), bf16[8,384,256]{1,2,0:T(8,128)(2,1)}, u32[]{:S(2)}, u32[]{:S(2)}) async-start(bf16[8,384,256]{1,2,0:T(8,128)(2,1)} %broadcast_in_dim.46), calls=%async_computation | async-start | bytes 3145728 | tf_op jit(solution)/shard_map/all_to_all | solution.py:49
  264.5 9.1 %copy-start.5 = (f32[2,672]{1,0:T(2,128)S(1)}, f32[2,672]{1,0:T(2,128)}, u32[]{:S(2)}) copy-start(f32[2,672]{1,0:T(2,128)} %param.24) | copy-start | bytes 16132
  270.2 9.5 %all-to-all-start.1 = ((f32[8,1,384]{2,1,0:T(1,128)}), f32[8,1,384]{2,1,0:T(1,128)S(1)}, u32[]{:S(2)}, u32[]{:S(2)}) async-start(f32[8,1,384]{2,1,0:T(1,128)} %broadcast_in_dim.48), calls=%async_computation.1 | async-start | bytes 24576 | tf_op jit(solution)/shard_map/all_to_all | solution.py:49
  273.6 67.0 %all-gather.11.cloned.1.call-start = ((), (), s32[]{:S(2)}) async-start(), calls=%async_computation.7 | async-start | bytes 5160960 | tf_op jit(solution)/shard_map/all_gather | solution.py:31
  340.6 3.4 copy-start.1
  348.5 22.8 %copy-start.2 = (bf16[256,5376]{1,0:T(8,128)(2,1)S(1)}, bf16[256,5376]{1,0:T(8,128)(2,1)}, u32[]{:S(2)}) copy-start(bf16[256,5376]{1,0:T(8,128)(2,1)} %copy.92) | copy-start | bytes 8257540
  348.5 31.3 %collective-permute-start.6 = (bf16[384,128]{1,0:T(8,128)(2,1)S(1)}, bf16[384,128]{1,0:T(8,128)(2,1)S(1)}, u32[]{:S(2)}, u32[]{:S(2)}) collective-permute-start(bf16[384,128]{1,0:T(8,128)(2,1)S(1)} %fusion.50), channel_id=1, source_target_pairs={{0,24},{8,32},{16,40},{24,48},{32,56},{40,64},{48,72},{56,80},{64,... | collective-permute-start | bytes 294920 | tf_op jit(solution)/shard_map/ppermute | solution.py:38
  351.4 28.3 %collective-permute-start.7 = (bf16[384,128]{1,0:T(8,128)(2,1)S(1)}, bf16[384,128]{1,0:T(8,128)(2,1)S(1)}, u32[]{:S(2)}, u32[]{:S(2)}) collective-permute-start(bf16[384,128]{1,0:T(8,128)(2,1)S(1)} %fusion.50), channel_id=1, source_target_pairs={{0,16},{8,24},{16,32},{24,40},{32,48},{40,56},{48,64},{56,72},{64,... | collective-permute-start | bytes 294920 | tf_op jit(solution)/shard_map/ppermute | solution.py:38
  359.5 13.9 %collective-permute-start.10 = (bf16[384,128]{0,1:T(8,128)(2,1)S(1)}, bf16[384,128]{0,1:T(8,128)(2,1)S(1)}, u32[]{:S(2)}, u32[]{:S(2)}) collective-permute-start(bf16[384,128]{0,1:T(8,128)(2,1)S(1)} %pad_maximum_fusion.2), channel_id=1, source_target_pairs={{0,16},{8,24},{16,32},{24,40},{32,48},{40,56},{48,64},{56,72},{64,... | collective-permute-start | bytes 294920 | tf_op jit(solution)/shard_map/ppermute | solution.py:38
  362.6 15.2 %collective-permute-start.11 = (bf16[384,128]{0,1:T(8,128)(2,1)S(1)}, bf16[384,128]{0,1:T(8,128)(2,1)S(1)}, u32[]{:S(2)}, u32[]{:S(2)}) collective-permute-start(bf16[384,128]{0,1:T(8,128)(2,1)S(1)} %pad_maximum_fusion.2), channel_id=1, source_target_pairs={{0,8},{8,16},{16,24},{24,32},{32,40},{40,48},{48,56},{56,64},{64,7... | collective-permute-start | bytes 294920 | tf_op jit(solution)/shard_map/ppermute | solution.py:38
  367.3 10.5 %collective-permute-start.9 = (bf16[384,128]{0,1:T(8,128)(2,1)S(1)}, bf16[384,128]{0,1:T(8,128)(2,1)S(1)}, u32[]{:S(2)}, u32[]{:S(2)}) collective-permute-start(bf16[384,128]{0,1:T(8,128)(2,1)S(1)} %pad_maximum_fusion.2), channel_id=1, source_target_pairs={{0,24},{8,32},{16,40},{24,48},{32,56},{40,64},{48,72},{56,80},{64,... | collective-permute-start | bytes 294920 | tf_op jit(solution)/shard_map/ppermute | solution.py:38
  371.3 6.5 %copy-start.3 = (pred[384,1536]{0,1:T(8,128)(4,1)S(1)}, pred[384,1536]{0,1:T(8,128)(4,1)}, u32[]{:S(2)}) copy-start(pred[384,1536]{0,1:T(8,128)(4,1)} %get-tuple-element.19) | copy-start | bytes 1769476
  373.3 9.0 %collective-permute-start.8 = (bf16[384,128]{1,0:T(8,128)(2,1)S(1)}, bf16[384,128]{1,0:T(8,128)(2,1)S(1)}, u32[]{:S(2)}, u32[]{:S(2)}) collective-permute-start(bf16[384,128]{1,0:T(8,128)(2,1)S(1)} %fusion.50), channel_id=1, source_target_pairs={{0,8},{8,16},{16,24},{24,32},{32,40},{40,48},{48,56},{56,64},{64,7... | collective-permute-start | bytes 294920 | tf_op jit(solution)/shard_map/ppermute | solution.py:38
  383.8 6.5 %copy-start.7 = (s32[2,16,42]{2,1,0:T(8,128)S(1)}, s32[2,16,42]{2,1,0:T(8,128)}, u32[]{:S(2)}) copy-start(s32[2,16,42]{2,1,0:T(8,128)} %param.22) | copy-start | bytes 16132
  385.1 24.6 %all-to-all-start.2 = ((bf16[8,384,256]{1,2,0:T(8,128)(2,1)}), bf16[8,384,256]{1,2,0:T(8,128)(2,1)S(1)}, u32[]{:S(2)}, u32[]{:S(2)}) async-start(bf16[8,384,256]{1,2,0:T(8,128)(2,1)} %broadcast_in_dim.54), calls=%async_computation.2 | async-start | bytes 3145728 | tf_op jit(solution)/shard_map/all_to_all | solution.py:49
Sparse Core Ops, SparseCore 0:
  23.1 51.5 all-gather.4
  77.2 86.2 all-gather.6
  166.1 77.7 all-gather.8
  291.5 48.9 all-gather.10
where the time goes:
time: 431 us; the launch traced here: 430 us
  waiting for transfers between devices  225 us (52%)
  starting transfers between devices  59.8 us (14%)
  matrix products  43.4 us (10%)
  blocking collectives  35.2 us (8%)
  local copies, waits for them, and re-layouts  29.7 us (7%)
  other arithmetic  23.4 us (5%)
  between operations  13.8 us (3%)
    all_gather x1, waiting for transfers between devices, in_one_piece(): lax.all_gather(both, axis, axis=dim, tiled=True)  85.7 us
    all_gather x2, waiting for transfers between devices, gather_axes(): nearer = lax.all_gather(array, axes[-1], axis=dim, tiled=True)  84.7 us
    ppermute x12, starting transfers between devices, passed_along(): return lax.ppermute(array, axis, pairs)  46.9 us
    all_to_all x3, waiting for transfers between devices, sent_to_all(): return lax.all_to_all(copies, axis, split_axis=0, concat_axis=0, tiled=True)  39.5 us
    all_gather x2, blocking collectives, gather_axes(): nearer = lax.all_gather(array, axes[-1], axis=dim, tiled=True)  26.5 us
    ppermute x12, waiting for transfers between devices, passed_along(): return lax.ppermute(array, axis, pairs)  14.1 us
    broadcast_in_dim x2, local copies, waits for them, and re-layouts, expand_scales(): jnp.repeat(jnp.repeat(factor, BLOCK, axis=0), BLOCK, axis=1)  13.6 us
    all_to_all x3, starting transfers between devices, sent_to_all(): return lax.all_to_all(copies, axis, split_axis=0, concat_axis=0, tiled=True)  12.8 us
  transfers between devices with their start and end apart: 19, of which 8 were waited for; matrix products, arithmetic and copies ran while one was open for 17% of the time, Pallas kernels for 0%

commit v1 on v0

v1 whole, which is shorter than its diff:
```python
import jax
import jax.numpy as jnp
from jax import lax
from jax.experimental import pallas as pl
from jax.experimental.pallas import tpu as pltpu
from jax.sharding import PartitionSpec as P

HD = 128
BLOCK = 128
LAYERS = 2
NSEQ = 32
NWGT = 8
TOK = 384
WIDTH = 672
ROWS = 168
D = 5376
MESH = pl.DeviceIdType.MESH

eps = 1e-06
query_scale = 168.0 ** (-0.5)
rope_base = 10000.0
BF = jnp.bfloat16
F32 = jnp.float32


def contract_rows(a, b):
    return lax.dot_general(a, b, (((0,), (0,)), ((), ())), preferred_element_type=F32)


def kernel(
    hid, wa, wb, wo, gin, gpost, qg, kg, cosine, sine, windows,
    out,
    H, WA, WB, O, MX, KV, SS, acc, Q, SC, PB, proj,
    w_recv, o_recv, h_recv, mx_recv, kv_recv, sib_recv, ss_recv, send,
):
    s = lax.axis_index("seq")
    w = lax.axis_index("wgt")
    core = s % 2
    y = (s // 2) % 4
    zh = s // 8
    x = w // 2
    zl = w % 2

    def seq_of(dz, dy):
        return ((zh + dz) % 4) * 8 + ((y + dy) % 4) * 2 + core

    def wgt_of(dx, dz):
        return ((x + dx) % 4) * 2 + (zl + dz) % 2

    sibling = s + 1 - 2 * core

    def on_seq(i):
        return {"seq": i, "wgt": w}

    def on_wgt(i):
        return {"seq": s, "wgt": i}

    def copy(src, dst, send_sem, recv_sem, device):
        return pltpu.make_async_remote_copy(
            src_ref=src,
            dst_ref=dst,
            send_sem=send_sem,
            recv_sem=recv_sem,
            device_id=device,
            device_id_type=MESH,
        )

    here = on_seq(sibling)

    def arrived(dst, sem):
        copy(dst, dst, send.at[0, 0], sem, here).wait_recv()

    def sent(region, sem):
        copy(region, region, sem, w_recv.at[0, 0, 0, 0], here).wait_send()

    def w_slot(l, half, index):
        if half == 0:
            return WA.at[l, index]
        if half == 1:
            return WB.at[l, index]
        return O.at[l, 2 * index + (half - 2)]

    def w_sem(l, half, dz, dy):
        if half < 2:
            return w_recv.at[l, half, dz, dy]
        return o_recv.at[l, half - 2, dz, dy]

    def w_to(l, half, owner, rel, step):
        slot = w_slot(l, half, owner)
        to = ((rel[0] - step[0]) % 4, (rel[1] - step[1]) % 4)
        copy(
            slot, slot, send.at[l, half], w_sem(l, half, *to), on_seq(seq_of(*step))
        ).start()

    def w_to_sibling(l, half, owner):
        slot = w_slot(l, half, owner)
        copy(slot, slot, send.at[l, half], sib_recv.at[l, half], here).start()

    def w_own(l, halves):
        for half in halves:
            for step in ((0, 1), (0, 3), (1, 0), (3, 0)):
                w_to(l, half, s, (0, 0), step)
            w_to_sibling(l, half, s)

    def w_event(l, half, dz, dy):
        owner = seq_of(dz, dy)
        arrived(w_slot(l, half, owner), w_sem(l, half, dz, dy))
        first = half % 2 == 0
        if dy == 0:
            w_to(l, half, owner, (dz, 0), (0, 1))
            w_to(l, half, owner, (dz, 0), (0, 3))
            if dz == 3 and first:
                w_to(l, half, owner, (3, 0), (1, 0))
            if dz == 1 and not first:
                w_to(l, half, owner, (1, 0), (3, 0))
        elif dy == 3 and first:
            w_to(l, half, owner, (dz, 3), (0, 1))
        elif dy == 1 and not first:
            w_to(l, half, owner, (dz, 1), (0, 3))
        w_to_sibling(l, half, owner)

    def h_to(l, piece, rel, step):
        slot = H.at[l, 4 * wgt_of(*rel) + piece]
        to = ((rel[0] - step[0]) % 4, (rel[1] - step[1]) % 2)
        copy(
            slot, slot, send.at[l, 4], h_recv.at[l, to[0], to[1], piece], on_wgt(wgt_of(*step))
        ).start()

    def h_wait(l, piece, dx, dz):
        arrived(H.at[l, 4 * wgt_of(dx, dz) + piece], h_recv.at[l, dx, dz, piece])

    def h_event(l, piece, dx, dz):
        h_wait(l, piece, dx, dz)
        if (dx, dz) == (0, 1):
            h_to(l, piece, (0, 1), (1, 0))
            h_to(l, piece, (0, 1), (3, 0))
        elif dx == 3 and piece < 2:
            h_to(l, piece, (3, dz), (1, 0))
        elif dx == 1 and piece >= 2:
            h_to(l, piece, (1, dz), (3, 0))

    def m_to(l, head, rel, step):
        slot = MX.at[l, wgt_of(*rel), head]
        to = ((rel[0] - step[0]) % 4, (rel[1] - step[1]) % 2)
        copy(
            slot, slot, send.at[l, 5], mx_recv.at[l, to[0], to[1], head], on_wgt(wgt_of(*step))
        ).start()

    def m_event(l, head, dx, dz):
        arrived(MX.at[l, wgt_of(dx, dz), head], mx_recv.at[l, dx, dz, head])
        if (dx, dz) == (0, 1):
            m_to(l, head, (0, 1), (1, 0))
            m_to(l, head, (0, 1), (3, 0))
        elif dx == 3 and head == 0:
            m_to(l, head, (3, dz), (1, 0))
        elif dx == 1 and head == 1:
            m_to(l, head, (1, dz), (3, 0))

    peers = [(dx, dz) for dz in range(2) for dx in range(4) if (dx, dz) != (0, 0)]

    def share_squares(l, kind, row):
        SS[l, kind, w] = jnp.broadcast_to(row, (8, TOK))
        slot = SS.at[l, kind, w]
        for rel in peers:
            copy(
                slot, slot, send.at[l, 6 + kind], ss_recv.at[l, kind], on_wgt(wgt_of(*rel))
            ).start()

    def all_squares(l, kind):
        arrived(SS.at[l, kind, pl.ds(0, 7)], ss_recv.at[l, kind])
        return jnp.sum(SS[l, kind], axis=0)[0:1]

    for l in range(LAYERS):
        WA[l, s] = wa[l]
        WB[l, s] = wb[l]
        for half in range(2):
            O[l, 2 * s + half] = wo[l, half]
    out[...] = hid[...]

    barrier = pltpu.get_barrier_semaphore()
    neighbours = [here]
    neighbours += [on_seq(seq_of(*step)) for step in ((0, 1), (0, 3), (1, 0), (3, 0))]
    neighbours += [on_wgt(wgt_of(*rel)) for rel in peers]
    after = on_seq((s + 2) % NSEQ)
    neighbours += [after, on_seq((s + NSEQ - 2) % NSEQ)]
    neighbours += [on_seq((s + NSEQ - 3 + 6 * core) % NSEQ)]
    for device in neighbours:
        pl.semaphore_signal(barrier, inc=1, device_id=device, device_id_type=MESH)
    pl.semaphore_wait(barrier, len(neighbours))

    w_own(0, (0, 1))

    def layer(l, carry):
        squares = jnp.zeros((1, TOK), F32)
        for i in range(4):
            state = out[i].astype(F32)
            H[l, 4 * w + i] = (state * gin[l, i]).astype(BF)
            squares += jnp.sum(state * state, axis=0, keepdims=True)
        for i in range(4):
            h_to(l, (0, 3, 1, 2)[i], (0, 0), (0, 1))
            h_to(l, i, (0, 0), (1, 0))
            h_to(l, 3 - i, (0, 0), (3, 0))
        share_squares(l, 0, squares)
        acc[...] = jnp.zeros_like(acc)

        timed = []
        for i in range(4):
            timed.append((3 * (i + 1), h_event, i, 3, 0))
            timed.append((3 * (i + 1), h_event, 3 - i, 1, 0))
            timed.append((5 * (i + 1), h_event, (0, 3, 1, 2)[i], 0, 1))
        for t, i in ((14, 0), (14, 3), (19.5, 1), (19.5, 2)):
            timed.append((t, h_event, i, 2, 0))
        for t, i in ((17, 0), (22.5, 3)):
            timed.append((t, h_event, i, 3, 1))
            timed.append((t, h_event, i, 1, 1))

        def w_times(t_own, t_z, t_opp, t_diag, t_z2, t_last, half0):
            events = []
            for k in range(2):
                half = half0 + k
                events += [(t_own[k], w_event, half, 0, 3), (t_own[k], w_event, half, 0, 1)]
                events += [(t_z[k], w_event, half, 3, 0), (t_z[k], w_event, half, 1, 0)]
                events += [(t_opp, w_event, half, 0, 2)]
                for dz in (3, 1):
                    events += [(t_diag[k], w_event, half, dz, 3), (t_diag[k], w_event, half, dz, 1)]
                    events += [(t_last[0], w_event, half, dz, 2)]
                events += [(t_z2, w_event, half, 2, 0)]
                events += [(t_last[1], w_event, half, 2, 3), (t_last[1], w_event, half, 2, 1)]
                events += [(t_last[2], w_event, half, 2, 2)]
            return events

        timed += w_times((2, 4), (4.5, 9), 6.2, (9.5, 13), 14.5, (16.5, 19, 22), 0)
        timed.sort(key=lambda e: e[0])
        for _, event, *which in timed:
            event(l, *which)
        w_own(l, (2, 3))
        for half, buf in ((0, WA), (1, WB)):
            arrived(buf.at[l, pl.ds(0, 16)], sib_recv.at[l, half])

        def multiply(t, carry):
            group = t // 4
            k = group % 4
            index = 4 * wgt_of(k * (k + 1) // 2, group // 4) + t % 4
            piece = H[l, index]
            acc[0:256] += contract_rows(WA[l, index], piece)
            acc[256:512] += contract_rows(WB[l, index], piece)
            return carry

        def while_arriving(j, carry):
            lax.fori_loop(10 * j, 10 * j + 10, multiply, 0)
            for dx in (3, 1):
                h_wait(l, 1 + j, dx, 1)

            @pl.when(j == 0)
            def _():
                h_to(l, 1, (3, 1), (1, 0))

            @pl.when(j == 1)
            def _():
                h_to(l, 2, (1, 1), (3, 0))

            return carry

        lax.fori_loop(0, 2, while_arriving, 0)
        o_events = w_times((1, 1), (2, 2), 3, (4, 4), 5, (6, 7, 8), 2)
        o_events.sort(key=lambda e: e[0])
        for t, event, *which in o_events:
            if t <= 2:
                event(l, *which)
        lax.fori_loop(20, 28, multiply, 0)

        def last_pieces(j, carry):
            high = j // 2
            odd = j % 2
            piece = (1 - high) * 3 * odd + high * (1 + odd)
            h_wait(l, piece, 2, 1)
            return multiply(28 + piece, carry)

        lax.fori_loop(0, 4, last_pieces, 0)

        row = lax.rsqrt(all_squares(l, 0) / D + eps)

        def head_of(rows, gain):
            values = acc[rows] * row
            values *= lax.rsqrt(jnp.mean(values * values, axis=0, keepdims=True) + eps)
            values *= gain[l]
            first = values[0:64]
            second = values[64:128]
            c = cosine[...]
            n = sine[...]
            return first * c - second * n, second * c + first * n

        first, second = head_of(pl.ds(256, 128), kg)
        KV[l, 3, 0:64] = first.astype(BF)
        KV[l, 3, 64:128] = second.astype(BF)
        KV[l, 3, 128:256] = (acc[384:512] * row).astype(BF)

        def kv_full(slot):
            copy(
                KV.at[l, slot], KV.at[l, 1], send.at[l, 8], kv_recv.at[l, 1], after
            ).start()

        def kv_sibling(slot):
            copy(
                KV.at[l, slot], KV.at[l, 2], send.at[l, 9], kv_recv.at[l, 2], here
            ).start()

        late = pl.ds(128, 256)

        def kv_far(slot, device):
            copy(
                KV.at[l, slot, :, late],
                KV.at[l, 0, :, late],
                send.at[l, 10],
                kv_recv.at[l, 0],
                device,
            ).start()

        kv_full(3)

        @pl.when(core == 0)
        def _():
            kv_sibling(3)

        @pl.when(core == 1)
        def _():
            kv_far(3, on_seq((s + 3) % NSEQ))

        for h in range(2):
            first, second = head_of(pl.ds(128 * h, 128), qg)
            Q[h, 0:64] = (first * query_scale).astype(BF)
            Q[h, 64:128] = (second * query_scale).astype(BF)

        arrived(KV.at[l, 1], kv_recv.at[l, 1])

        @pl.when(core == 0)
        def _():
            kv_far(1, here)

        @pl.when(core == 1)
        def _():
            kv_sibling(1)

        for t, event, *which in o_events:
            if 2 < t <= 5:
                event(l, *which)
        arrived(KV.at[l, 2], kv_recv.at[l, 2])
        arrived(KV.at[l, 0, :, late], kv_recv.at[l, 0])

        window = windows[l]

        def attend(h, carry):
            SC[128:384] = contract_rows(KV[l, 0, 0:128, 128:384], Q[h])
            for j in range(1, 4):
                SC[384 * j : 384 * (j + 1)] = contract_rows(KV[l, j, 0:128], Q[h])

            def soften(c, carry):
                lanes = pl.ds(pl.multiple_of(128 * c, 128), 128)
                keys = lax.broadcasted_iota(jnp.int32, (1408, 128), 0) + 128
                gap = lax.broadcasted_iota(jnp.int32, (1408, 128), 1) + 128 * c + 1152 - keys
                allowed = (gap >= 0) & (gap < window) & (keys >= 1152 - TOK * s)
                scores = jnp.where(allowed, SC[128:1536, lanes], -1e30)
                scores = jnp.exp(scores - jnp.max(scores, axis=0, keepdims=True))
                total = jnp.sum(scores, axis=0, keepdims=True)
                PB[128:1536, lanes] = (scores * (1.0 / total)).astype(BF)
                return carry

            lax.fori_loop(0, 3, soften, 0)
            mixed = jnp.dot(
                KV[l, 0, 128:256, 128:384], PB[128:384], preferred_element_type=F32
            )
            for j in range(1, 4):
                mixed += jnp.dot(
                    KV[l, j, 128:256], PB[384 * j : 384 * (j + 1)], preferred_element_type=F32
                )
            MX[l, w, h] = mixed.astype(BF)
            for step in ((0, 1), (1, 0), (3, 0)):
                m_to(l, h, (0, 0), step)
            return carry

        lax.fori_loop(0, 2, attend, 0)

        for t, event, *which in o_events:
            if t > 5:
                event(l, *which)
        for head in range(2):
            m_event(l, head, 3, 0)
            m_event(l, head, 1, 0)
            m_event(l, head, 0, 1)
        for head in range(2):
            m_event(l, head, 2, 0)
        for head in range(2):
            m_event(l, head, 3, 1)
            m_event(l, head, 1, 1)
        arrived(O.at[l, pl.ds(0, 16)], sib_recv.at[l, 2])
        arrived(O.at[l, pl.ds(0, 16)], sib_recv.at[l, 3])
        proj[...] = jnp.zeros_like(proj)

        def project(t, carry):
            k = t % 4
            index = wgt_of(k * (k + 1) // 2, t // 4)
            block = O[l, pl.ds(8 * index, 8)].reshape(256, WIDTH)
            proj[...] += contract_rows(block, MX[l, index].reshape(256, TOK))
            return carry

        lax.fori_loop(0, 7, project, 0)
        m_event(l, 0, 2, 1)
        m_event(l, 1, 2, 1)
        lax.fori_loop(7, 8, project, 0)

        squares = jnp.zeros((1, TOK), F32)
        for i in range(4):
            part = proj[ROWS * i : ROWS * (i + 1)]
            squares += jnp.sum(part * part, axis=0, keepdims=True)
        share_squares(l, 1, squares)

        @pl.when(l == 0)
        def _():
            w_own(1, (0, 1))

        row = lax.rsqrt(all_squares(l, 1) / D + eps)
        for i in range(4):
            post = proj[ROWS * i : ROWS * (i + 1)] * row * gpost[l, i]
            out[i] = (out[i].astype(F32) + post).astype(BF)

        sent(WA.at[l, pl.ds(0, 31)], send.at[l, 0])
        sent(WB.at[l, pl.ds(0, 31)], send.at[l, 1])
        sent(O.at[l, pl.ds(0, 31)], send.at[l, 2])
        sent(O.at[l, pl.ds(0, 31)], send.at[l, 3])
        sent(H.at[l, pl.ds(0, 28)], send.at[l, 4])
        sent(MX.at[l, pl.ds(0, 7)], send.at[l, 5])
        for kind in range(2):
            sent(SS.at[l, kind, pl.ds(0, 7)], send.at[l, 6 + kind])
        sent(KV.at[l, 1], send.at[l, 8])
        sent(KV.at[l, 2], send.at[l, 9])
        sent(KV.at[l, 0, :, late], send.at[l, 10])
        return carry

    lax.fori_loop(0, LAYERS, layer, 0)


def row_factors(scale_codes, first_row, rows):
    blocks = (first_row + jnp.arange(rows, dtype=jnp.int32)) // BLOCK
    pick = blocks[:, None] == jnp.arange(scale_codes.shape[1], dtype=jnp.int32)[None, :]
    factor = jnp.exp2(scale_codes.astype(F32) - 127.0)
    return jnp.sum(jnp.where(pick[None, :, :, None], factor[:, None], 0.0), axis=2)


def per_device(
    hidden,
    q_weight,
    k_weight,
    v_weight,
    o_weight,
    q_scale,
    k_scale,
    v_scale,
    o_scale,
    in_gain,
    post_gain,
    q_gain,
    k_gain,
    windows,
):
    s = lax.axis_index("seq")
    w = lax.axis_index("wgt")
    scales = jnp.concatenate([q_scale, k_scale, v_scale], axis=2)
    factors = jnp.repeat(row_factors(scales, ROWS * s, ROWS), BLOCK, axis=2).astype(BF)
    wa = q_weight * factors[:, :, :256]
    wb = jnp.concatenate([k_weight, v_weight], axis=2) * factors[:, :, 256:]
    o_rows = jnp.exp2(
        lax.dynamic_slice_in_dim(o_scale, s // 2, 1, axis=1).astype(F32) - 127.0
    )
    columns = (w * WIDTH + jnp.arange(WIDTH, dtype=jnp.int32)) // BLOCK
    pick = columns[:, None] == jnp.arange(D // BLOCK, dtype=jnp.int32)[None, :]
    o_factor = jnp.sum(jnp.where(pick[None], o_rows, 0.0), axis=2).astype(BF)
    wo = (o_weight * o_factor[:, None, :]).reshape(LAYERS, 2, 32, WIDTH)
    gin = lax.dynamic_slice_in_dim(in_gain, w * WIDTH, WIDTH, axis=1)
    gin = gin.reshape(LAYERS, 4, ROWS, 1)
    gpost = post_gain.reshape(LAYERS, 4, ROWS, 1)
    half = HD // 2
    position = s * TOK + jnp.arange(TOK, dtype=jnp.int32)
    inverse = rope_base ** (-jnp.arange(half, dtype=F32) * 2.0 / HD)
    angles = inverse[:, None] * position.astype(F32)[None, :]
    hid = hidden.T.reshape(4, ROWS, TOK)

    vmem = pl.BlockSpec(memory_space=pltpu.VMEM)
    dma = pltpu.SemaphoreType.DMA
    state = pl.pallas_call(
        kernel,
        out_shape=jax.ShapeDtypeStruct((4, ROWS, TOK), BF),
        in_specs=[vmem] * 10 + [pl.BlockSpec(memory_space=pltpu.SMEM)],
        out_specs=vmem,
        scratch_shapes=[
            pltpu.VMEM((LAYERS, 32, ROWS, TOK), BF),
            pltpu.VMEM((LAYERS, NSEQ, ROWS, 256), BF),
            pltpu.VMEM((LAYERS, NSEQ, ROWS, 256), BF),
            pltpu.VMEM((LAYERS, 2 * NSEQ, 32, WIDTH), BF),
            pltpu.VMEM((LAYERS, NWGT, 2, HD, TOK), BF),
            pltpu.VMEM((LAYERS, 4, 2 * HD, TOK), BF),
            pltpu.VMEM((LAYERS, 2, NWGT, 8, TOK), F32),
            pltpu.VMEM((512, TOK), F32),
            pltpu.VMEM((2, HD, TOK), BF),
            pltpu.VMEM((4 * TOK, TOK), F32),
            pltpu.VMEM((4 * TOK, TOK), BF),
            pltpu.VMEM((WIDTH, TOK), F32),
            dma((LAYERS, 2, 4, 4)),
            dma((LAYERS, 2, 4, 4)),
            dma((LAYERS, 4, 2, 4)),
            dma((LAYERS, 4, 2, 2)),
            dma((LAYERS, 3)),
            dma((LAYERS, 4)),
            dma((LAYERS, 2)),
            dma((LAYERS, 11)),
        ],
        compiler_params=pltpu.CompilerParams(
            collective_id=0, has_side_effects=True, vmem_limit_bytes=60 * 1024 * 1024
        ),
    )(
        hid,
        wa,
        wb,
        wo,
        gin,
        gpost,
        q_gain.reshape(LAYERS, HD, 1),
        k_gain.reshape(LAYERS, HD, 1),
        jnp.cos(angles),
        jnp.sin(angles),
        windows,
    )
    return state.reshape(WIDTH, TOK).T


def solution(mesh):
    in_specs = (
        P("seq", "wgt"),
        P(None, "seq", "wgt"),
        P(None, "seq", "wgt"),
        P(None, "seq", "wgt"),
        P(None, "seq", "wgt"),
        P(None, None, "wgt"),
        P(None, None, "wgt"),
        P(None, None, "wgt"),
        P(),
        P(),
        P(None, "wgt"),
        P(),
        P(),
        P(),
    )
    return jax.shard_map(
        per_device, mesh=mesh, in_specs=in_specs, out_specs=P("seq", "wgt"), check_vma=False
    )
```

time: 431 us -> 202 us (0.47)
  waiting for transfers between devices: 225 us -> 0 us
  Pallas kernels: 0 us -> 186 us
  starting transfers between devices: 59.8 us -> 0 us
  matrix products: 43.4 us -> 0 us
  blocking collectives: 35.2 us -> 0 us
  local copies, waits for them, and re-layouts: 29.7 us -> 8.98 us
  other arithmetic: 23.4 us -> 3.86 us
  between operations: 13.8 us -> 0.14 us
    pallas_call x0 -> x1, Pallas kernels: none -> 186 us  [per_device(): pl.pallas_call(kernel, out_shape=jax.ShapeDtypeStruct((4, ROWS, TOK), BF)...]
    all_gather x4 -> x0, waiting for transfers between devices: 170 us -> none  [the longest x1 85.7 us: in_one_piece(): lax.all_gather(both, axis, axis=dim, tiled=True)]
    ppermute x12 -> x0, starting transfers between devices: 46.9 us -> none  [passed_along(): return lax.ppermute(array, axis, pairs)]
    dot_general x14 -> x0, matrix products: 43.4 us -> none  [the longest x2 11.2 us: per_device(): jnp.dot(normed, gathered[1][layer_idx] * tables[1], preferred_element_typ...]
    all_to_all x3 -> x0, waiting for transfers between devices: 39.5 us -> none  [sent_to_all(): return lax.all_to_all(copies, axis, split_axis=0, concat_axis=0, tiled=True)]
    all_gather x2 -> x0, blocking collectives: 26.5 us -> none  [gather_axes(): nearer = lax.all_gather(array, axes[-1], axis=dim, tiled=True)]
    broadcast_in_dim x10 -> x2, local copies, waits for them, and re-layouts: 17.6 us -> 0.52 us  [the longest x1 0.42 us: per_device(): jnp.repeat(row_factors(scales, ROWS * s, ROWS), BLOCK, axis=2).astype(BF)]
    ppermute x12 -> x0, waiting for transfers between devices: 14.1 us -> none  [passed_along(): return lax.ppermute(array, axis, pairs)]
  transfers between devices with their start and end apart: 19 -> 0, of which waited for: 8 -> 0; matrix products, arithmetic and copies ran while one was open for 17% -> 0% of each run, Pallas kernels for 0% -> 0%
where the time goes in v1:
time: 202 us; the launch traced here: 199 us
  Pallas kernels  186 us (92%)
  local copies, waits for them, and re-layouts  8.98 us (4%)
  other arithmetic  3.86 us (2%)
    pallas_call x1, Pallas kernels, per_device(): pl.pallas_call(kernel, out_shape=jax.ShapeDtypeStruct((4, ROWS, TOK), BF)...  186 us

profile of v1, /device:TPU:64, one launch (start us, length us, event | category | flops | bytes accessed | tf_op | source)
XLA Modules:
  0.0 198.9 jit_solution(771485014266918492)
XLA Ops:
  0.0 0.7 multiply_exponential_fusion
  0.8 0.0 copy-start.6
  0.8 0.0 copy-start.9
  0.8 0.0 copy-start.10
  0.8 0.6 copy-done.6
  1.4 0.0 copy-done.9
  1.5 0.0 copy-done.10
  1.5 0.1 constant_dynamic-slice_fusion
  1.6 0.1 copy.23
  1.7 0.2 select_reduce_fusion.1
  2.0 0.0 copy-start.7
  2.0 0.1 copy.21
  2.1 0.2 select_reduce_fusion
  2.3 0.2 copy.22
  2.4 0.2 copy-done.7
  2.7 0.8 copy.26.qg
  3.5 0.8 copy.27.kg
  4.3 0.7 broadcast_multiply_fusion
  5.0 1.1 multiply_sine_fusion
  6.1 0.4 broadcast_in_dim.58
  6.5 0.0 copy-start.2
  6.5 0.0 copy-start.3
  6.5 0.0 copy-start.4
  6.5 0.1 convert_element_type.33
  6.7 0.7 copy-done.2
  7.4 0.1 copy-done.3
  7.5 0.0 copy-done.4
  7.5 0.8 slice_multiply_fusion
  8.4 1.4 reshape.148.gin
  9.7 1.4 reshape.149.gpost
  11.1 185.9 %shard_map.136 = bf16[4,168,384]{2,1,0:T(8,128)(2,1)} custom-call(bf16[4,168,384]{2,1,0:T(8,128)(2,1)} %bitcast.12, bf16[2,168,256]{2,1,0:T(8,128)(2,1)} %get-tuple-element.6.wa, bf16[2,168,256]{2,1,0:T(8,128)(2,1)} %get-tuple-element.5.wb, bf16[2,2,32,672]{3,2,1,0:T(8,128)(2,1)} %bitcast.11, f32[2,4,168,1]{3,2,1,0:T(8,128)} %reshape.148.gin, ...), custom_call_target="tpu_custom_call" | custom-call | tf_op jit(solution)/shard_map/pallas_call | solution.py:489
  197.0 1.9 copy.29
  (15 shorter events, 0.1 us)
Async XLA Ops:
  0.0 1.5 copy-start
  0.8 0.7 copy-start.6
  0.8 0.7 copy-start.9
  0.8 0.7 copy-start.10
  2.0 0.7 copy-start.7
  2.1 2.2 %copy-start.1 = (bf16[2,64,672]{2,1,0:T(8,128)(2,1)S(1)}, bf16[2,64,672]{2,1,0:T(8,128)(2,1)}, u32[]{:S(2)}) copy-start(bf16[2,64,672]{2,1,0:T(8,128)(2,1)} %param.18) | copy-start | bytes 516100
  2.7 0.8 copy-start.8
  6.5 0.9 copy-start.2
  6.5 1.0 copy-start.3
  6.5 1.0 copy-start.4
  8.3 1.4 copy-start.5

commit v2 on v1

v2 whole, which is shorter than its diff:
```python
import jax
import jax.numpy as jnp
from jax import lax
from jax.experimental import pallas as pl
from jax.experimental.pallas import tpu as pltpu
from jax.sharding import PartitionSpec as P

HD = 128
BLOCK = 128
LAYERS = 2
NSEQ = 32
NWGT = 8
TOK = 384
WIDTH = 672
ROWS = 168
D = 5376
MESH = pl.DeviceIdType.MESH

eps = 1e-06
query_scale = 168.0 ** (-0.5)
rope_base = 10000.0
H_BY_Z = ((1, 2), (0, 1, 2, 3))
BF = jnp.bfloat16
F32 = jnp.float32


def contract_rows(a, b):
    return lax.dot_general(a, b, (((0,), (0,)), ((), ())), preferred_element_type=F32)


FIRST_HOPS = 8.2


def w_schedule(half0):
    events = []
    for k in range(2):
        half = half0 + k
        if half0 == 0:
            own, zs, opp, last = (2.5, 4.3)[k], (4.4, 8.2)[k], 6.2, ((19, 20.8)[k], 22.7)
            diag, edge, z2 = ((8.3, 9.7), (11.6, 13.4))[k], (15.5, 17.2), 11.6
        else:
            own, zs, opp, last = 1, 2, 3, (6, 7)
            diag, edge, z2 = (4, 4), (6, 6), 5
        events += [(own, half, 0, 3), (own, half, 0, 1), (opp, half, 0, 2)]
        for i, dz in enumerate((3, 1)):
            events += [(zs, half, dz, 0), (diag[i], half, dz, 3), (diag[i], half, dz, 1)]
            events += [(edge[i], half, dz, 2)]
        events += [(z2, half, 2, 0), (last[0], half, 2, 3), (last[0], half, 2, 1)]
        events += [(last[1], half, 2, 2)]
    return sorted(events, key=lambda e: e[0])


def kernel(
    hid, wa, wb, wo, gains, cosine, sine, windows,
    out,
    H, WA, WB, O, MX, KV, SS, acc, Q, KX, SC, PB, TOT, MIX, RB, proj,
    w_recv, o_recv, h_recv, mx_recv, kv_recv, sib_recv, ss_recv, send,
):
    s = lax.axis_index("seq")
    w = lax.axis_index("wgt")
    core = s % 2
    y = (s // 2) % 4
    zh = s // 8
    x = w // 2
    zl = w % 2

    def seq_of(dz, dy):
        return ((zh + dz) % 4) * 8 + ((y + dy) % 4) * 2 + core

    def wgt_of(dx, dz):
        return ((x + dx) % 4) * 2 + (zl + dz) % 2

    sibling = s + 1 - 2 * core

    def on_seq(i):
        return {"seq": i, "wgt": w}

    def on_wgt(i):
        return {"seq": s, "wgt": i}

    def copy(src, dst, send_sem, recv_sem, device):
        return pltpu.make_async_remote_copy(
            src_ref=src,
            dst_ref=dst,
            send_sem=send_sem,
            recv_sem=recv_sem,
            device_id=device,
            device_id_type=MESH,
        )

    here = on_seq(sibling)

    def arrived(dst, sem):
        copy(dst, dst, send.at[0, 0], sem, here).wait_recv()

    def sent(region, sem):
        copy(region, region, sem, w_recv.at[0, 0, 0, 0], here).wait_send()

    def w_slot(l, half, index):
        if half == 0:
            return WA.at[l, index]
        if half == 1:
            return WB.at[l, index]
        return O.at[l, 2 * index + (half - 2)]

    def w_sem(l, half, dz, dy):
        if half < 2:
            return w_recv.at[l, half, dz, dy]
        return o_recv.at[l, half - 2, dz, dy]

    def w_to(l, half, owner, rel, step):
        slot = w_slot(l, half, owner)
        to = ((rel[0] - step[0]) % 4, (rel[1] - step[1]) % 4)
        copy(
            slot, slot, send.at[l, half], w_sem(l, half, *to), on_seq(seq_of(*step))
        ).start()

    def w_to_sibling(l, half, owner):
        slot = w_slot(l, half, owner)
        copy(slot, slot, send.at[l, half], sib_recv.at[l, half], here).start()

    def w_own(l, halves):
        for half in halves:
            for step in ((0, 1), (0, 3), (1, 0), (3, 0)):
                w_to(l, half, s, (0, 0), step)
            w_to_sibling(l, half, s)

    def w_event(l, half, dz, dy):
        owner = seq_of(dz, dy)
        arrived(w_slot(l, half, owner), w_sem(l, half, dz, dy))
        first = half % 2 == 0
        if dy == 0:
            if dz == 3 and first:
                w_to(l, half, owner, (3, 0), (1, 0))
            if dz == 1 and not first:
                w_to(l, half, owner, (1, 0), (3, 0))
            w_to(l, half, owner, (dz, 0), (0, 1))
            w_to(l, half, owner, (dz, 0), (0, 3))
        elif dy == 3 and first:
            w_to(l, half, owner, (dz, 3), (0, 1))
        elif dy == 1 and not first:
            w_to(l, half, owner, (dz, 1), (0, 3))
        w_to_sibling(l, half, owner)

    def h_to(l, piece, rel, step):
        slot = H.at[l, 4 * wgt_of(*rel) + piece]
        to = ((rel[0] - step[0]) % 4, (rel[1] - step[1]) % 2)
        copy(
            slot, slot, send.at[l, 4], h_recv.at[l, to[0], to[1], piece], on_wgt(wgt_of(*step))
        ).start()

    def h_event(l, piece, dx, dz):
        arrived(H.at[l, 4 * wgt_of(dx, dz) + piece], h_recv.at[l, dx, dz, piece])
        if (dx, dz) == (0, 1):
            h_to(l, piece, (0, 1), (1, 0))
            h_to(l, piece, (0, 1), (3, 0))
        elif (dx, dz) == (2, 0):
            if piece in H_BY_Z[l]:
                h_to(l, piece, (2, 0), (0, 1))
        elif dz == 1 and piece in H_BY_Z[l]:
            pass
        elif dx == 3 and piece < 2:
            h_to(l, piece, (3, dz), (1, 0))
        elif dx == 1 and piece >= 2:
            h_to(l, piece, (1, dz), (3, 0))

    def m_to(l, head, rel, step):
        slot = MX.at[l, wgt_of(*rel), head]
        to = ((rel[0] - step[0]) % 4, (rel[1] - step[1]) % 2)
        copy(
            slot, slot, send.at[l, 5], mx_recv.at[l, to[0], to[1], head], on_wgt(wgt_of(*step))
        ).start()

    def m_event(l, head, dx, dz):
        arrived(MX.at[l, wgt_of(dx, dz), head], mx_recv.at[l, dx, dz, head])
        if (dx, dz) == (0, 1):
            m_to(l, head, (0, 1), (1, 0))
            m_to(l, head, (0, 1), (3, 0))
        elif (dx, dz) == (2, 0):
            m_to(l, head, (2, 0), (0, 1))
        elif (dx, dz, head) == (3, 0, 0):
            m_to(l, head, (3, 0), (1, 0))
        elif (dx, dz, head) == (1, 0, 1):
            m_to(l, head, (1, 0), (3, 0))

    peers = [(dx, dz) for dz in range(2) for dx in range(4) if (dx, dz) != (0, 0)]

    def share_squares(l, kind, row):
        SS[l, kind, w] = row
        slot = SS.at[l, kind, w]
        for rel in peers:
            copy(
                slot, slot, send.at[l, 6 + kind], ss_recv.at[l, kind], on_wgt(wgt_of(*rel))
            ).start()

    def all_squares(l, kind):
        arrived(SS.at[l, kind, pl.ds(0, 7)], ss_recv.at[l, kind])
        return jnp.sum(SS[l, kind], axis=0)

    def gain(l, kind, rows):
        return gains[rows, 2 * kind + l : 2 * kind + l + 1]

    for l in range(LAYERS):
        WA[l, s] = wa[l]
        WB[l, s] = wb[l]
        for half in range(2):
            O[l, 2 * s + half] = wo[l, half]
        for slot in range(3):
            KV[l, slot] = jnp.zeros((2, HD, TOK), BF)
    out[...] = hid[...]

    barrier = pltpu.get_barrier_semaphore()
    neighbours = [here]
    neighbours += [on_seq(seq_of(*step)) for step in ((0, 1), (0, 3), (1, 0), (3, 0))]
    neighbours += [on_wgt(wgt_of(*rel)) for rel in peers]
    after = on_seq((s + 2) % NSEQ)
    neighbours += [after, on_seq((s + NSEQ - 2) % NSEQ)]
    neighbours += [on_seq((s + NSEQ - 3 + 6 * core) % NSEQ)]
    for device in neighbours:
        pl.semaphore_signal(barrier, inc=1, device_id=device, device_id_type=MESH)
    pl.semaphore_wait(barrier, len(neighbours))

    w_own(0, (0, 1))

    def layer(l):
        squares = jnp.zeros((1, TOK), F32)
        for i in range(4):
            state = out[i].astype(F32)
            H[l, 4 * w + i] = (state * gain(l, 0, pl.ds(ROWS * i, ROWS))).astype(BF)
            squares += jnp.sum(state * state, axis=0, keepdims=True)
        for i in range(4):
            h_to(l, i, (0, 0), (1, 0))
            h_to(l, 3 - i, (0, 0), (3, 0))
        share_squares(l, 0, squares)
        acc[...] = jnp.zeros_like(acc)

        def multiply(group, carry):
            k = group % 4
            first = 4 * wgt_of(k * (k + 1) // 2, group // 4)
            for buf, rows in ((WA, pl.ds(0, 256)), (WB, pl.ds(256, 256))):
                total = acc[rows]
                for i in range(4):
                    total += contract_rows(buf[l, first + i], H[l, first + i])
                acc[rows] = total
            return carry

        def weights_here():
            for half, buf in ((0, WA), (1, WB)):
                arrived(buf.at[l, pl.ds(0, 16)], sib_recv.at[l, half])

        timed = []

        def at(t, step, *args):
            timed.append((t, step, args))

        if l == 0:
            for t, *which in w_schedule(0):
                at(t, w_event, l, *which)
            at(24.4, weights_here)
        else:
            for t, *which in w_schedule(0):
                if t > FIRST_HOPS:
                    at(max(t - 7.5, 1), w_event, l, *which)
            at(17.1, weights_here)
            for t, *which in w_schedule(2):
                at((0, 17.15, 18, 19, 20.6, 21.5, 26.1, 28.6)[t], w_event, l, *which)

        def h_own_by_z():
            for i in (0, 3, 1, 2):
                h_to(l, i, (0, 0), (0, 1))

        if l == 0:
            pair = (14.2, 17, 19.7, 22.5)
            far = (14.2, 14.2, 17, 17)
            late_x = (19.9, 22.5, 25.4, 28.1)
            late_z = (29.5, 29.5, 29.5, 29.5)
            at(8.25, h_own_by_z)
            at(21, w_own, l, (2, 3))
            blocks = ((24.5, 0, 3), (25.5, 3, 5), (28.2, 5, 7), (29.6, 7, 8))
        else:
            pair = (3.2, 6, 8.8, 11.5)
            far = (14.5, 14.5, 20, 20)
            late_x = (17.2, 22.8, 25.6, 28.4)
            late_z = (20.5, 20.5, 25.7, 25.7)
            at(0, h_own_by_z)
            at(11.5, w_own, l, (2, 3))
            blocks = ((17.2, 0, 3), (20.4, 3, 5), (26, 7, 8), (28.5, 5, 7))
        for i in range(4):
            near = (3.2, 6, 8.8, 11.5)[i]
            piece = (0, 3, 1, 2)[i]
            at(near, h_event, l, i, 3, 0)
            at(near, h_event, l, 3 - i, 1, 0)
            at(pair[i], h_event, l, piece, 0, 1)
            at(far[i], h_event, l, piece, 2, 0)
            at(late_x[i], h_event, l, piece, 3, 1)
            at(late_x[i], h_event, l, piece, 1, 1)
            at(late_z[i], h_event, l, piece, 2, 1)

        def multiply_groups(first, last):
            lax.fori_loop(first, last, multiply, 0)

        for t, first, last in blocks:
            at(t, multiply_groups, first, last)
        timed.sort(key=lambda e: e[0])
        for _, step, args in timed:
            step(*args)

        def o_event(*stages):
            if l == 0:
                for t, *which in w_schedule(2):
                    if t in stages:
                        w_event(l, *which)

        o_event(1)
        row = lax.rsqrt(all_squares(l, 0) / D + eps)

        def head_of(rows, kind):
            values = acc[rows] * row
            values *= lax.rsqrt(jnp.mean(values * values, axis=0, keepdims=True) + eps)
            values *= gain(l, kind, pl.ds(WIDTH, HD))
            first = values[0:64]
            second = values[64:128]
            c = cosine[...]
            n = sine[...]
            return first * c - second * n, second * c + first * n

        late = pl.ds(128, 256)

        def kv_full(part):
            copy(
                KV.at[l, 3, part], KV.at[l, 1, part],
                send.at[l, 8], kv_recv.at[l, 1, part], after,
            ).start()

        def kv_sibling(slot, part):
            copy(
                KV.at[l, slot, part], KV.at[l, 2, part],
                send.at[l, 9], kv_recv.at[l, 2, part], here,
            ).start()

        def kv_far(slot, part, device):
            copy(
                KV.at[l, slot, part, :, late], KV.at[l, 0, part, :, late],
                send.at[l, 10], kv_recv.at[l, 0, part], device,
            ).start()

        def kv_own(part):
            direct = s < NSEQ - 2
            if part == 1:
                direct &= y != 3

                @pl.when((y == 3) & (s < NSEQ - 2))
                def _():
                    for half in range(2):
                        rows = pl.ds(64 * half, 64)
                        copy(
                            KV.at[l, 3, 1, rows], RB.at[l, rows],
                            send.at[l, 8], kv_recv.at[l, 3, half], on_seq(s - 6),
                        ).start()

            @pl.when(direct)
            def _():
                kv_full(part)

            @pl.when(core == 0)
            def _():
                kv_sibling(3, part)

        first, second = head_of(pl.ds(256, 128), 1)
        KV[l, 3, 0, 0:64] = first.astype(BF)
        KV[l, 3, 0, 64:128] = second.astype(BF)
        kv_own(0)
        KV[l, 3, 1] = (acc[384:512] * row).astype(BF)
        kv_own(1)

        for h in range(2):
            first, second = head_of(pl.ds(128 * h, 128), 0)
            Q[h, 0:64] = (first * query_scale).astype(BF)
            Q[h, 64:128] = (second * query_scale).astype(BF)

        window = windows[l]

        def attend(slot):
            skip = 128 if slot == 0 else 0
            rows = TOK - skip
            KX[0:rows] = KV[l, slot, 0, :, skip:TOK].T

            def one_head(h, carry):
                SC[0:rows] = jnp.dot(KX[0:rows], Q[h], preferred_element_type=F32)
                keys = lax.broadcasted_iota(jnp.int32, (rows, 128), 0) + (TOK * slot + skip)
                for c in range(3):
                    lanes = pl.ds(128 * c, 128)
                    gap = lax.broadcasted_iota(jnp.int32, (rows, 128), 1) + (
                        128 * c + 3 * TOK
                    ) - keys
                    allowed = (gap < window) & (keys >= 3 * TOK - TOK * s)
                    if slot == 3:
                        allowed &= gap >= 0
                    weight = jnp.where(allowed, jnp.exp(SC[0:rows, lanes]), 0.0)
                    total = jnp.sum(weight, axis=0, keepdims=True)
                    if slot != 3:
                        total += TOT[h, :, lanes]
                    TOT[h, :, lanes] = total
                    PB[0:rows, lanes] = weight.astype(BF)
                mixed = jnp.dot(
                    KV[l, slot, 1, :, skip:TOK], PB[0:rows], preferred_element_type=F32
                )
                if slot != 3:
                    mixed += MIX[h]
                MIX[h] = mixed
                return carry

            lax.fori_loop(0, 2, one_head, 0)

        o_event(2, 3)
        attend(3)

        @pl.when((core == 1) & (s < NSEQ - 3))
        def _():
            for part in range(2):
                kv_far(3, part, on_seq((s + 3) % NSEQ))

        @pl.when((y == 0) & (s < NSEQ - 8))
        def _():
            for half in range(2):
                rows = pl.ds(64 * half, 64)
                arrived(RB.at[l, rows], kv_recv.at[l, 3, half])
                copy(
                    RB.at[l, rows], KV.at[l, 1, 1, rows],
                    send.at[l, 11], kv_recv.at[l, 1, 1], on_seq(s + 8),
                ).start()

        o_event(4, 5)
        for part in range(2):

            @pl.when(s >= 2)
            def _():
                arrived(KV.at[l, 1, part], kv_recv.at[l, 1, part])

            @pl.when((core == 0) & (s >= 2))
            def _():
                kv_far(1, part, here)

            @pl.when((core == 1) & (s >= 2))
            def _():
                kv_sibling(1, part)

        attend(1)

        @pl.when(s >= 1)
        def _():
            for part in range(2):
                arrived(KV.at[l, 2, part], kv_recv.at[l, 2, part])

        attend(2)

        @pl.when(s >= 3)
        def _():
            for part in range(2):
                arrived(KV.at[l, 0, part, :, late], kv_recv.at[l, 0, part])

        attend(0)
        for h in range(2):
            MX[l, w, h] = (MIX[h] * (1.0 / TOT[h])).astype(BF)
            for step in ((0, 1), (1, 0), (3, 0)):
                m_to(l, h, (0, 0), step)

        proj[...] = jnp.zeros_like(proj)

        def project(group, carry):
            k = group % 4
            index = wgt_of(k * (k + 1) // 2, group // 4)
            block = O[l, pl.ds(8 * index, 8)].reshape(256, WIDTH)
            proj[...] += contract_rows(block, MX[l, index].reshape(256, TOK))
            return carry

        m_event(l, 0, 3, 0)
        m_event(l, 1, 1, 0)
        m_event(l, 0, 0, 1)
        o_event(6)
        m_event(l, 1, 3, 0)
        m_event(l, 0, 1, 0)
        m_event(l, 1, 0, 1)
        if l == 0:
            w_own(1, (0, 1))
        m_event(l, 0, 2, 0)
        m_event(l, 1, 2, 0)
        o_event(7)
        arrived(O.at[l, pl.ds(0, 16)], sib_recv.at[l, 2])
        arrived(O.at[l, pl.ds(0, 16)], sib_recv.at[l, 3])
        lax.fori_loop(0, 5, project, 0)
        for head in range(2):
            m_event(l, head, 3, 1)
            m_event(l, head, 1, 1)
        lax.fori_loop(5, 7, project, 0)
        m_event(l, 0, 2, 1)
        m_event(l, 1, 2, 1)
        lax.fori_loop(7, 8, project, 0)

        squares = jnp.zeros((1, TOK), F32)
        for i in range(4):
            part = proj[ROWS * i : ROWS * (i + 1)]
            squares += jnp.sum(part * part, axis=0, keepdims=True)
        share_squares(l, 1, squares)

        if l == 0:
            for t, *which in w_schedule(0):
                if t <= FIRST_HOPS:
                    w_event(1, *which)
        row = lax.rsqrt(all_squares(l, 1) / D + eps)
        for i in range(4):
            post = proj[ROWS * i : ROWS * (i + 1)] * row * gain(l, 1, pl.ds(ROWS * i, ROWS))
            out[i] = (out[i].astype(F32) + post).astype(BF)

        sent(WA.at[l, pl.ds(0, 31)], send.at[l, 0])
        sent(WB.at[l, pl.ds(0, 31)], send.at[l, 1])
        sent(O.at[l, pl.ds(0, 31)], send.at[l, 2])
        sent(O.at[l, pl.ds(0, 31)], send.at[l, 3])
        sent(H.at[l, pl.ds(0, 28)], send.at[l, 4])
        sent(MX.at[l, pl.ds(0, 7)], send.at[l, 5])
        for kind in range(2):
            sent(SS.at[l, kind, pl.ds(0, 7)], send.at[l, 6 + kind])

        @pl.when(s < NSEQ - 2)
        def _():
            sent(KV.at[l, 1], send.at[l, 8])

        @pl.when((y == 0) & (s < NSEQ - 8))
        def _():
            sent(RB.at[l], send.at[l, 11])

        @pl.when((core == 0) | (s >= 2))
        def _():
            sent(KV.at[l, 2], send.at[l, 9])

        @pl.when(((core == 0) & (s >= 2)) | ((core == 1) & (s < NSEQ - 3)))
        def _():
            sent(KV.at[l, 0, :, :, late], send.at[l, 10])


    for l in range(LAYERS):
        layer(l)


def row_factors(scale_codes, first_row, rows):
    blocks = (first_row + jnp.arange(rows, dtype=jnp.int32)) // BLOCK
    pick = blocks[:, None] == jnp.arange(scale_codes.shape[1], dtype=jnp.int32)[None, :]
    factor = jnp.exp2(scale_codes.astype(F32) - 127.0)
    return jnp.sum(jnp.where(pick[None, :, :, None], factor[:, None], 0.0), axis=2)


def per_device(
    hidden,
    q_weight,
    k_weight,
    v_weight,
    o_weight,
    q_scale,
    k_scale,
    v_scale,
    o_scale,
    in_gain,
    post_gain,
    q_gain,
    k_gain,
    windows,
):
    s = lax.axis_index("seq")
    w = lax.axis_index("wgt")
    scales = jnp.concatenate([q_scale, k_scale, v_scale], axis=2)
    factors = jnp.repeat(row_factors(scales, ROWS * s, ROWS), BLOCK, axis=2).astype(BF)
    wa = q_weight * factors[:, :, :256]
    wb = jnp.concatenate([k_weight, v_weight], axis=2) * factors[:, :, 256:]
    o_rows = jnp.exp2(
        lax.dynamic_slice_in_dim(o_scale, s // 2, 1, axis=1).astype(F32) - 127.0
    )
    columns = (w * WIDTH + jnp.arange(WIDTH, dtype=jnp.int32)) // BLOCK
    pick = columns[:, None] == jnp.arange(D // BLOCK, dtype=jnp.int32)[None, :]
    o_factor = jnp.sum(jnp.where(pick[None], o_rows, 0.0), axis=2).astype(BF)
    wo = (o_weight * o_factor[:, None, :]).reshape(LAYERS, 2, 32, WIDTH)
    gin = lax.dynamic_slice_in_dim(in_gain, w * WIDTH, WIDTH, axis=1)
    gains = jnp.concatenate(
        [
            jnp.concatenate([gin, post_gain, jnp.zeros((4, WIDTH), F32)], axis=0),
            jnp.concatenate([q_gain, k_gain, jnp.zeros((4, HD), F32)], axis=0),
        ],
        axis=1,
    ).T
    half = HD // 2
    position = s * TOK + jnp.arange(TOK, dtype=jnp.int32)
    inverse = rope_base ** (-jnp.arange(half, dtype=F32) * 2.0 / HD)
    angles = inverse[:, None] * position.astype(F32)[None, :]
    hid = hidden.T.reshape(4, ROWS, TOK)

    vmem = pl.BlockSpec(memory_space=pltpu.VMEM)
    dma = pltpu.SemaphoreType.DMA
    state = pl.pallas_call(
        kernel,
        out_shape=jax.ShapeDtypeStruct((4, ROWS, TOK), BF),
        in_specs=[vmem] * 7 + [pl.BlockSpec(memory_space=pltpu.SMEM)],
        out_specs=vmem,
        scratch_shapes=[
            pltpu.VMEM((LAYERS, 32, ROWS, TOK), BF),
            pltpu.VMEM((LAYERS, NSEQ, ROWS, 256), BF),
            pltpu.VMEM((LAYERS, NSEQ, ROWS, 256), BF),
            pltpu.VMEM((LAYERS, 2 * NSEQ, 32, WIDTH), BF),
            pltpu.VMEM((LAYERS, NWGT, 2, HD, TOK), BF),
            pltpu.VMEM((LAYERS, 4, 2, HD, TOK), BF),
            pltpu.VMEM((LAYERS, 2, NWGT, 1, TOK), F32),
            pltpu.VMEM((512, TOK), F32),
            pltpu.VMEM((2, HD, TOK), BF),
            pltpu.VMEM((TOK, HD), BF),
            pltpu.VMEM((TOK, TOK), F32),
            pltpu.VMEM((TOK, TOK), BF),
            pltpu.VMEM((2, 1, TOK), F32),
            pltpu.VMEM((2, HD, TOK), F32),
            pltpu.VMEM((LAYERS, HD, TOK), BF),
            pltpu.VMEM((WIDTH, TOK), F32),
            dma((LAYERS, 2, 4, 4)),
            dma((LAYERS, 2, 4, 4)),
            dma((LAYERS, 4, 2, 4)),
            dma((LAYERS, 4, 2, 2)),
            dma((LAYERS, 4, 2)),
            dma((LAYERS, 4)),
            dma((LAYERS, 2)),
            dma((LAYERS, 12)),
        ],
        compiler_params=pltpu.CompilerParams(
            collective_id=0, has_side_effects=True, vmem_limit_bytes=44 * 1024 * 1024
        ),
    )(
        hid,
        wa,
        wb,
        wo,
        gains,
        jnp.cos(angles),
        jnp.sin(angles),
        windows,
    )
    return state.reshape(WIDTH, TOK).T


def solution(mesh):
    in_specs = (
        P("seq", "wgt"),
        P(None, "seq", "wgt"),
        P(None, "seq", "wgt"),
        P(None, "seq", "wgt"),
        P(None, "seq", "wgt"),
        P(None, None, "wgt"),
        P(None, None, "wgt"),
        P(None, None, "wgt"),
        P(),
        P(),
        P(None, "wgt"),
        P(),
        P(),
        P(),
    )
    return jax.shard_map(
        per_device, mesh=mesh, in_specs=in_specs, out_specs=P("seq", "wgt"), check_vma=False
    )
```

time: 202 us -> 167 us (0.83)
  Pallas kernels: 186 us -> 158 us
  local copies, waits for them, and re-layouts: 8.98 us -> 4.94 us
    pallas_call x1, Pallas kernels: 186 us -> 158 us  [per_device(): pl.pallas_call(kernel, out_shape=jax.ShapeDtypeStruct((4, ROWS, TOK), BF)...]
    reshape x4 -> x0, local copies, waits for them, and re-layouts: 4.34 us -> none  [the longest x1 1.38 us: per_device(): gpost = post_gain.reshape(LAYERS, 4, ROWS, 1)]
where the time goes in v2:
time: 167 us; the launch traced here: 165 us
  Pallas kernels  158 us (95%)
  local copies, waits for them, and re-layouts  4.94 us (3%)
  other arithmetic  1.85 us (1%)
    pallas_call x1, Pallas kernels, per_device(): pl.pallas_call(kernel, out_shape=jax.ShapeDtypeStruct((4, ROWS, TOK), BF)...  158 us
    unnamed x27, local copies, waits for them, and re-layouts  3.76 us

profile of v2, /device:TPU:64, one launch (start us, length us, event | category | flops | bytes accessed | tf_op | source)
XLA Modules:
  0.0 165.1 jit_solution(13881786972488495761)
XLA Ops:
  0.0 0.7 multiply_exponential_fusion
  0.8 0.0 copy-start.8
  0.8 0.0 copy-start.11
  0.8 0.0 copy-start.12
  0.8 0.6 copy-done.8
  1.4 0.0 copy-done.11
  1.5 0.0 copy-done.12
  1.5 0.1 constant_dynamic-slice_fusion
  1.6 0.0 copy-start.9
  1.6 0.0 copy-start.10
  1.7 0.6 copy-done.7
  2.3 0.0 copy-done.10
  2.3 0.1 maximum_maximum_fusion
  2.4 0.1 copy.24
  2.5 0.2 select_reduce_fusion.1
  2.8 0.1 copy.22
  2.9 0.2 select_reduce_fusion
  3.1 0.2 copy.23
  3.2 0.0 copy-done.3
  3.3 0.4 multiply_sine_fusion
  3.7 0.4 broadcast_in_dim.64
  4.1 0.0 copy-start.4
  4.2 0.0 copy-start.6
  4.2 0.1 convert_element_type.33
  4.3 0.7 copy-done.4
  5.1 0.1 copy-done.5
  5.1 0.0 copy-done.6
  5.2 0.1 slice_multiply_fusion
  5.3 0.2 copy.25
  5.5 0.7 copy-done.1
  6.2 158.1 %shard_map.136 = bf16[4,168,384]{2,1,0:T(8,128)(2,1)S(1)} custom-call(bf16[4,168,384]{2,1,0:T(8,128)(2,1)S(1)} %bitcast.12, bf16[2,168,256]{2,1,0:T(8,128)(2,1)S(1)} %get-tuple-element.6.wa, bf16[2,168,256]{2,1,0:T(8,128)(2,1)S(1)} %get-tuple-element.5.wb, bf16[2,2,32,672]{3,2,1,0:T(8,128)(2,1)S(1)} %bitcast.11, f32[800,8]{1,0:T(8,128)S(1)} %bitcast.10, ...), custom_call_target="tpu_custom_call" | custom-call | tf_op jit(solution)/shard_map/pallas_call | solution.py:597
  164.3 0.8 copy.27
  (19 shorter events, 0.1 us)
Async XLA Ops:
  0.0 1.5 copy-start
  0.8 0.7 copy-start.8
  0.8 0.7 copy-start.11
  0.8 0.7 copy-start.12
  1.6 0.7 copy-start.7
  1.6 0.7 copy-start.9
  1.6 0.7 copy-start.10
  2.3 0.9 copy-start.3
  4.1 0.9 copy-start.4
  4.1 1.0 copy-start.5
  4.2 1.0 copy-start.6
  5.2 1.0 copy-start.1
  5.4 0.8 copy-start.2

commit v3 on v1

v3 whole, which is shorter than its diff:
```python
import jax
import jax.numpy as jnp
from jax import lax
from jax.experimental import pallas as pl
from jax.experimental.pallas import tpu as pltpu
from jax.sharding import PartitionSpec as P

HD = 128
BLOCK = 128
LAYERS = 2
NSEQ = 32
NWGT = 8
TOK = 384
WIDTH = 672
ROWS = 168
D = 5376
MESH = pl.DeviceIdType.MESH

eps = 1e-06
query_scale = 168.0 ** (-0.5)
rope_base = 10000.0
BF = jnp.bfloat16
F32 = jnp.float32


def contract_rows(a, b):
    return lax.dot_general(a, b, (((0,), (0,)), ((), ())), preferred_element_type=F32)


Y_US = {"w": 1.9, "o": 1.08, "k": 2.15}
Z_US = {"w": 3.8, "o": 2.15}
X_US = {"h": 2.85, "m": 1.1}
ZP_US = {"h": 2.85, "m": 1.1}
LAT = {"y": 2.2, "z": 2.8, "x": 2.2, "p": 2.2}
H_BY_Z = ((1, 2), (0, 1, 2, 3))


def w_forwards(half, dz, dy):
    first = half in (1, 2)
    steps = []
    if dy == 0:
        if dz == 3 and first:
            steps.append((1, 0))
        if dz == 1 and not first:
            steps.append((3, 0))
        steps += [(0, 1), (0, 3)]
    elif dy == 3 and first:
        steps.append((0, 1))
    elif dy == 1 and not first:
        steps.append((0, 3))
    return steps


def a_forwards(by_z, piece, dx, dz):
    if (dx, dz) == (0, 1):
        return [(1, 0), (3, 0)]
    if (dx, dz) == (2, 0):
        return [(0, 1)] if piece in by_z else []
    if dz == 1 and piece in by_z:
        return []
    if dx == 3 and piece < 2:
        return [(1, 0)]
    if dx == 1 and piece >= 2:
        return [(3, 0)]
    return []


M_BY_Z = ((1, 2), (1, 2))
BY_Z = {"h": H_BY_Z, "m": M_BY_Z}


SLACK = ((0.5, 1.0), (4.0, 4.0))


def schedule():
    free = {}
    arrival = {}
    done = {}
    order = []
    now = 0.0

    def link(name, us, lat):
        free[name] = max(free.get(name, 0.0), now) + us
        return free[name] + lat

    def send_w(l, half, rel, step):
        kind = "w" if half < 2 else "o"
        to = ((rel[0] - step[0]) % 4, (rel[1] - step[1]) % 4)
        if step[0]:
            t = link("z" + str(step[0]), Z_US[kind], LAT["z"])
        else:
            t = link("y" + str(step[1]), Y_US[kind], LAT["y"])
        arrival["w", l, half, *to] = t

    def send_a(kind, l, piece, rel, step):
        to = ((rel[0] - step[0]) % 4, (rel[1] - step[1]) % 2)
        if step[0]:
            t = link("x" + str(step[0]), X_US[kind], LAT["x"])
        else:
            t = link("z1", ZP_US[kind], LAT["p"])
        arrival[kind, l, piece, *to] = t

    w_events = lambda l, half0: [("w", l, h, dz, dy) for h in (half0, half0 + 1) for dz in range(4) for dy in range(4) if (dz, dy) != (0, 0)]
    owner = lambda g: ([0, 1, 3, 2][g % 4], g // 4)

    tasks = {}
    for l in range(2):
        tasks["scale", l] = (0.3, [("fin", l - 1)] if l else [], 0)
        tasks["wown", l] = (0.05, [("att0", 0)] if l else [], 1)
        tasks["oown", l] = (0.05, ([("scale", 1)] if l else []) + [("w", l, h, dz, 0) for h in (0, 1) for dz in (1, 2, 3)], 1)
        tasks["hz", l] = (0.05, [("scale", l)] + [("w", l, h, dz, 0) for h in (0, 1) for dz in (1, 3)], 0)
        for half in (0, 1):
            name = ("wsib", l, half)
            tasks[name] = (0.02, [e for e in w_events(l, 0) if e[2] == half] + [("kvsent", 0) if (l, half) == (0, 0) else ("scale", l)], 2 - half)
            for g in range(8):
                ow = owner(g)
                pieces = [("scale", l)] if ow == (0, 0) else [("h", l, i, *ow) for i in range(4)]
                tasks["mm", l, half, g] = (0.45, [name] + pieces, 4 - half)
        tasks["kvsent", l] = (0.15, [("mm", l, 1, g) for g in range(8)], 0)
        tasks["heads", l] = (0.2, [("mm", l, 0, g) for g in range(8)] + [("kvsent", l)], 1)
        tasks["att3", l] = (1.07, [("heads", l)], 3)
        tasks["att1", l] = (1.12, [("att3", l), ("kv1", l)], 3)
        tasks["att2", l] = (1.12, [("att1", l), ("kv2", l)], 3)
        tasks["att0", l] = (1.1, [("att2", l), ("kv0", l)], 0)
        tasks["osib", l] = (0.02, w_events(l, 2) + [("att0", l)], 2)
        for g in range(8):
            ow = owner(g)
            tasks["pj", l, g] = (0.38, [("osib", l), ("att0", l)] + ([] if ow == (0, 0) else [("m", l, i, *ow) for i in range(4)]), 3)
        tasks["share", l] = (0.3, [("pj", l, g) for g in range(8)], 0)
        tasks["fin", l] = (0.3, [("share", l), ("ss", l)], 0)

    def run_task(name):
        nonlocal now
        kind, l = name[0], name[1]
        now += tasks[name][0]
        if kind == "wown":
            for h in (1, 0):
                for step in ((0, 1), (0, 3), (1, 0), (3, 0)):
                    send_w(l, h, (0, 0), step)
        if kind == "oown":
            for h in (2, 3):
                for step in ((0, 1), (0, 3), (1, 0), (3, 0)):
                    send_w(l, h, (0, 0), step)
        if kind == "scale":
            for i in range(4):
                send_a("h", l, i, (0, 0), (1, 0))
                send_a("h", l, 3 - i, (0, 0), (3, 0))
        if kind == "hz":
            for i in (0, 3, 1, 2):
                send_a("h", l, i, (0, 0), (0, 1))
        if kind == "kvsent":
            a = link("y1", Y_US["k"], 2.8)
            b = link("y1", Y_US["k"], 2.8)
            arrival["kv1", l] = b + 0.5
            arrival["kv2", l] = b + 2.3
            arrival["kv0", l] = b + 2.5
        if kind == "att0":
            for i in range(4):
                for piece, step in ((i, (1, 0)), (3 - i, (3, 0)), ((0, 3, 1, 2)[i], (0, 1))):
                    send_a("m", l, piece, (0, 0), step)
        if kind == "share":
            arrival["ss", l] = now + 4.0
        done[name] = now
        order.append(name)

    def run_event(ev):
        nonlocal now
        now += 0.06
        kind = ev[0]
        if kind == "w":
            _, l, half, dz, dy = ev
            for step in w_forwards(half, dz, dy):
                send_w(l, half, (dz, dy), step)
        elif kind in "hm":
            _, l, piece, dx, dz = ev
            for step in a_forwards(BY_Z[kind][l], piece, dx, dz):
                send_a(kind, l, piece, (dx, dz), step)
        done[ev] = now
        order.append(ev)

    def eff(ev):
        t = arrival[ev]
        if ev[0] == "w":
            return t + SLACK[ev[1]][ev[2] // 2]
        if ev[0] in "hm" and ev[3:] == (0, 1):
            return t + 0.5
        return t

    while True:
        pend = [e for e in arrival if e not in done]
        ready = [t for t in tasks if t not in done and all(d in done for d in tasks[t][1])]
        if not pend and not ready:
            break
        urgent = [t for t in ready if tasks[t][2] == 0]
        arrived = [e for e in pend if eff(e) <= now]
        if urgent:
            run_task(min(urgent))
        elif arrived:
            run_event(min(arrived, key=lambda e: (eff(e), e)))
        elif ready:
            run_task(min(ready, key=lambda t: (tasks[t][2], tasks[t][1] and max(done[d] for d in tasks[t][1]) or 0, t)))
        else:
            e = min(pend, key=lambda e: (eff(e), e))
            now = max(now, eff(e))
            run_event(e)
    return order


def kernel(
    hid, wa, wb, wo, gains, cosine, sine, windows,
    out,
    H, WA, WB, O, MX, KV, SS, acc, Q, ROW, KX, SC, PB, TOT, MIX, RB, proj,
    w_recv, o_recv, h_recv, mx_recv, kv_recv, sib_recv, ss_recv, send,
):
    s = lax.axis_index("seq")
    w = lax.axis_index("wgt")
    core = s % 2
    y = (s // 2) % 4
    zh = s // 8
    x = w // 2
    zl = w % 2

    def seq_of(dz, dy):
        return ((zh + dz) % 4) * 8 + ((y + dy) % 4) * 2 + core

    def wgt_of(dx, dz):
        return ((x + dx) % 4) * 2 + (zl + dz) % 2

    sibling = s + 1 - 2 * core

    def on_seq(i):
        return {"seq": i, "wgt": w}

    def on_wgt(i):
        return {"seq": s, "wgt": i}

    def copy(src, dst, send_sem, recv_sem, device):
        return pltpu.make_async_remote_copy(
            src_ref=src,
            dst_ref=dst,
            send_sem=send_sem,
            recv_sem=recv_sem,
            device_id=device,
            device_id_type=MESH,
        )

    here = on_seq(sibling)

    def arrived(dst, sem):
        copy(dst, dst, send.at[0, 0], sem, here).wait_recv()

    def sent(region, sem):
        copy(region, region, sem, w_recv.at[0, 0, 0, 0], here).wait_send()

    def w_slot(l, half, index):
        if half == 0:
            return WA.at[l, index]
        if half == 1:
            return WB.at[l, index]
        return O.at[l, 2 * index + (half - 2)]

    def w_sem(l, half, dz, dy):
        if half < 2:
            return w_recv.at[l, half, dz, dy]
        return o_recv.at[l, half - 2, dz, dy]

    def w_to(l, half, owner, rel, step):
        slot = w_slot(l, half, owner)
        to = ((rel[0] - step[0]) % 4, (rel[1] - step[1]) % 4)
        copy(
            slot, slot, send.at[l, half], w_sem(l, half, *to), on_seq(seq_of(*step))
        ).start()

    def w_to_sibling(l, half, owner):
        slot = w_slot(l, half, owner)
        copy(slot, slot, send.at[l, half], sib_recv.at[l, half], here).start()

    def w_own(l, halves, along="yz"):
        for half in halves:
            if "y" in along:
                w_to(l, half, s, (0, 0), (0, 1))
                w_to(l, half, s, (0, 0), (0, 3))
                w_to_sibling(l, half, s)
            if "z" in along:
                w_to(l, half, s, (0, 0), (1, 0))
                w_to(l, half, s, (0, 0), (3, 0))

    def w_event(l, half, dz, dy):
        owner = seq_of(dz, dy)
        arrived(w_slot(l, half, owner), w_sem(l, half, dz, dy))
        for step in w_forwards(half, dz, dy):
            w_to(l, half, owner, (dz, dy), step)
        w_to_sibling(l, half, owner)

    def h_to(l, piece, rel, step):
        slot = H.at[l, 4 * wgt_of(*rel) + piece]
        to = ((rel[0] - step[0]) % 4, (rel[1] - step[1]) % 2)
        copy(
            slot, slot, send.at[l, 4], h_recv.at[l, to[0], to[1], piece], on_wgt(wgt_of(*step))
        ).start()

    def m_to(l, piece, rel, step):
        slot = MX.at[l, wgt_of(*rel), piece]
        to = ((rel[0] - step[0]) % 4, (rel[1] - step[1]) % 2)
        copy(
            slot, slot, send.at[l, 5], mx_recv.at[l, to[0], to[1], piece], on_wgt(wgt_of(*step))
        ).start()

    def h_event(l, piece, dx, dz):
        arrived(H.at[l, 4 * wgt_of(dx, dz) + piece], h_recv.at[l, dx, dz, piece])
        for step in a_forwards(BY_Z["h"][l], piece, dx, dz):
            h_to(l, piece, (dx, dz), step)

    def m_event(l, piece, dx, dz):
        arrived(MX.at[l, wgt_of(dx, dz), piece], mx_recv.at[l, dx, dz, piece])
        for step in a_forwards(BY_Z["m"][l], piece, dx, dz):
            m_to(l, piece, (dx, dz), step)

    peers = [(dx, dz) for dz in range(2) for dx in range(4) if (dx, dz) != (0, 0)]

    def share_squares(l, kind, row):
        SS[l, kind, w] = row
        slot = SS.at[l, kind, w]
        for rel in peers:
            copy(
                slot, slot, send.at[l, 6 + kind], ss_recv.at[l, kind], on_wgt(wgt_of(*rel))
            ).start()

    def all_squares(l, kind):
        arrived(SS.at[l, kind, pl.ds(0, 7)], ss_recv.at[l, kind])
        return jnp.sum(SS[l, kind], axis=0)

    def gain(l, kind, rows):
        return gains[rows, 2 * kind + l : 2 * kind + l + 1]

    for l in range(LAYERS):
        WA[l, s] = wa[l]
        WB[l, s] = wb[l]
        for half in range(2):
            O[l, 2 * s + half] = wo[l, half]
        for slot in range(3):
            KV[l, slot] = jnp.zeros((2, HD, TOK), BF)
    out[...] = hid[...]

    barrier = pltpu.get_barrier_semaphore()
    neighbours = [here]
    neighbours += [on_seq(seq_of(*step)) for step in ((0, 1), (0, 3), (1, 0), (3, 0))]
    neighbours += [on_wgt(wgt_of(*rel)) for rel in peers]
    after = on_seq((s + 2) % NSEQ)
    neighbours += [after, on_seq((s + NSEQ - 2) % NSEQ)]
    neighbours += [on_seq((s + NSEQ - 3 + 6 * core) % NSEQ)]
    for device in neighbours:
        pl.semaphore_signal(barrier, inc=1, device_id=device, device_id_type=MESH)
    pl.semaphore_wait(barrier, len(neighbours))

    late = pl.ds(128, 256)

    def scale(l):
        squares = jnp.zeros((1, TOK), F32)
        for i in range(4):
            state = out[i].astype(F32)
            H[l, 4 * w + i] = (state * gain(l, 0, pl.ds(ROWS * i, ROWS))).astype(BF)
            squares += jnp.sum(state * state, axis=0, keepdims=True)
        for i in range(4):
            h_to(l, i, (0, 0), (1, 0))
            h_to(l, 3 - i, (0, 0), (3, 0))
        share_squares(l, 0, squares)
        acc[...] = jnp.zeros_like(acc)

    def multiply(l, half, first, last):
        buf, rows = ((WA, pl.ds(0, 256)), (WB, pl.ds(256, 256)))[half]

        def one(group, carry):
            k = group % 4
            index = 4 * wgt_of(k * (k + 1) // 2, group // 4)
            total = acc[rows]
            for i in range(4):
                total += contract_rows(buf[l, index + i], H[l, index + i])
            acc[rows] = total
            return carry

        lax.fori_loop(first, last, one, 0)

    def head_of(l, rows, row, kind):
        values = acc[rows] * row
        values *= lax.rsqrt(jnp.mean(values * values, axis=0, keepdims=True) + eps)
        values *= gain(l, kind, pl.ds(WIDTH, HD))
        first = values[0:64]
        second = values[64:128]
        c = cosine[...]
        n = sine[...]
        return first * c - second * n, second * c + first * n

    def kv_sibling(l, slot, part):
        copy(
            KV.at[l, slot, part], KV.at[l, 2, part],
            send.at[l, 9], kv_recv.at[l, 2, part], here,
        ).start()

    def kv_far(l, slot, part, device):
        copy(
            KV.at[l, slot, part, :, late], KV.at[l, 0, part, :, late],
            send.at[l, 10], kv_recv.at[l, 0, part], device,
        ).start()

    def kv_next(l, part, rows):
        copy(
            KV.at[l, 3, part, rows], KV.at[l, 1, part, rows],
            send.at[l, 8], kv_recv.at[l, 1, part], after,
        ).start()

    corner = [pl.ds(64 + 32 * i, 32) for i in range(2)]

    def keys_values(l):
        row = lax.rsqrt(all_squares(l, 0) / D + eps)
        ROW[...] = row
        KV[l, 3, 1] = (acc[384:512] * row).astype(BF)

        @pl.when((y == 3) & (s < NSEQ - 2))
        def _():
            for i in range(2):
                copy(
                    KV.at[l, 3, 1, corner[i]], RB.at[l, pl.ds(32 * i, 32)],
                    send.at[l, 8], kv_recv.at[l, 3, i], on_seq(s - 6),
                ).start()

        first, second = head_of(l, pl.ds(256, 128), row, 1)
        KV[l, 3, 0, 0:64] = first.astype(BF)
        KV[l, 3, 0, 64:128] = second.astype(BF)

        @pl.when(s < NSEQ - 2)
        def _():
            kv_next(l, 0, pl.ds(0, 128))
            kv_next(l, 1, pl.ds(0, 64))

        @pl.when((y != 3) & (s < NSEQ - 2))
        def _():
            kv_next(l, 1, pl.ds(64, 64))

        @pl.when(core == 0)
        def _():
            for part in range(2):
                kv_sibling(l, 3, part)

        @pl.when((core == 1) & (s < NSEQ - 3))
        def _():
            for part in range(2):
                kv_far(l, 3, part, on_seq((s + 3) % NSEQ))

    def queries(l):
        for h in range(2):
            first, second = head_of(l, pl.ds(128 * h, 128), ROW[...], 0)
            Q[h, 0:64] = (first * query_scale).astype(BF)
            Q[h, 64:128] = (second * query_scale).astype(BF)

    def attend(l, slot):
        skip = 128 if slot == 0 else 0
        rows = TOK - skip
        window = windows[l]
        KX[0:rows] = KV[l, slot, 0, :, skip:TOK].T
        keys = lax.broadcasted_iota(jnp.int32, (rows, 128), 0) + (TOK * slot + skip)
        for h in range(2):
            SC[h, 0:rows] = jnp.dot(KX[0:rows], Q[h], preferred_element_type=F32)
        for h in range(2):
            for c in range(3):
                lanes = pl.ds(128 * c, 128)
                gap = lax.broadcasted_iota(jnp.int32, (rows, 128), 1) + (128 * c + 3 * TOK) - keys
                allowed = (gap < window) & (keys >= 3 * TOK - TOK * s)
                if slot == 3:
                    allowed &= gap >= 0
                weight = jnp.where(allowed, jnp.exp(SC[h, 0:rows, lanes]), 0.0)
                total = jnp.sum(weight, axis=0, keepdims=True)
                if slot != 3:
                    total += TOT[h, :, lanes]
                TOT[h, :, lanes] = total
                PB[h, 0:rows, lanes] = weight.astype(BF)
            mixed = jnp.dot(
                KV[l, slot, 1, :, skip:TOK], PB[h, 0:rows], preferred_element_type=F32
            )
            if slot != 3:
                mixed += MIX[h]
            MIX[h] = mixed
        if slot == 0:
            for h in range(2):
                mixed = (MIX[h] * (1.0 / TOT[h])).astype(BF)
                MX[l, w, 2 * h] = mixed[0:64]
                MX[l, w, 2 * h + 1] = mixed[64:128]
            for i in range(4):
                for piece, step in ((i, (1, 0)), (3 - i, (3, 0)), ((0, 3, 1, 2)[i], (0, 1))):
                    m_to(l, piece, (0, 0), step)
            proj[...] = jnp.zeros_like(proj)

    def kv_event(l, slot):
        if slot == 1:

            @pl.when((y == 0) & (s < NSEQ - 8))
            def _():
                for i in range(2):
                    rows = RB.at[l, pl.ds(32 * i, 32)]
                    arrived(rows, kv_recv.at[l, 3, i])
                    copy(
                        rows, KV.at[l, 1, 1, corner[i]],
                        send.at[l, 11], kv_recv.at[l, 1, 1], on_seq(s + 8),
                    ).start()

            for part in range(2):

                @pl.when(s >= 2)
                def _():
                    arrived(KV.at[l, 1, part], kv_recv.at[l, 1, part])

                @pl.when((core == 0) & (s >= 2))
                def _():
                    kv_far(l, 1, part, here)

                @pl.when((core == 1) & (s >= 2))
                def _():
                    kv_sibling(l, 1, part)

        if slot == 2:

            @pl.when(s >= 1)
            def _():
                for part in range(2):
                    arrived(KV.at[l, 2, part], kv_recv.at[l, 2, part])

        if slot == 0:

            @pl.when(s >= 3)
            def _():
                for part in range(2):
                    arrived(KV.at[l, 0, part, :, late], kv_recv.at[l, 0, part])

    def project(l, first, last):
        def one(group, carry):
            k = group % 4
            index = wgt_of(k * (k + 1) // 2, group // 4)
            block = O[l, pl.ds(8 * index, 8)].reshape(256, WIDTH)
            proj[...] += contract_rows(block, MX[l, index].reshape(256, TOK))
            return carry

        lax.fori_loop(first, last, one, 0)

    def share(l):
        squares = jnp.zeros((1, TOK), F32)
        for i in range(4):
            part = proj[ROWS * i : ROWS * (i + 1)]
            squares += jnp.sum(part * part, axis=0, keepdims=True)
        share_squares(l, 1, squares)

    def finish(l):
        row = lax.rsqrt(all_squares(l, 1) / D + eps)
        for i in range(4):
            post = proj[ROWS * i : ROWS * (i + 1)] * row * gain(l, 1, pl.ds(ROWS * i, ROWS))
            out[i] = (out[i].astype(F32) + post).astype(BF)

    steps = []
    for name in schedule():
        if name[0] in ("mm", "pj"):
            *key, group = name
            if steps and steps[-1][:-2] == tuple(key) and steps[-1][-1] == group:
                steps[-1] = (*steps[-1][:-1], group + 1)
            else:
                steps.append((*key, group, group + 1))
        else:
            steps.append(name)

    for kind, l, *which in steps:
        if kind == "w":
            w_event(l, *which)
        elif kind == "h":
            h_event(l, *which)
        elif kind == "m":
            m_event(l, *which)
        elif kind == "mm":
            multiply(l, *which)
        elif kind == "pj":
            project(l, *which)
        elif kind == "scale":
            scale(l)
        elif kind == "wown":
            w_own(l, (1, 0))
        elif kind == "oown":
            w_own(l, (2, 3))
        elif kind == "hz":
            for i in (0, 3, 1, 2):
                h_to(l, i, (0, 0), (0, 1))
        elif kind == "wsib":
            half = which[0]
            arrived((WA, WB)[half].at[l, pl.ds(0, 16)], sib_recv.at[l, half])
        elif kind == "osib":
            for half in (2, 3):
                arrived(O.at[l, pl.ds(0, 16)], sib_recv.at[l, half])
        elif kind == "kvsent":
            keys_values(l)
        elif kind == "heads":
            queries(l)
        elif kind in ("kv0", "kv1", "kv2"):
            kv_event(l, int(kind[2]))
        elif kind in ("att0", "att1", "att2", "att3"):
            attend(l, int(kind[3]))
        elif kind == "share":
            share(l)
        elif kind == "fin":
            finish(l)

    for l in range(LAYERS):
        sent(WA.at[l, pl.ds(0, 31)], send.at[l, 0])
        sent(WB.at[l, pl.ds(0, 31)], send.at[l, 1])
        sent(O.at[l, pl.ds(0, 31)], send.at[l, 2])
        sent(O.at[l, pl.ds(0, 31)], send.at[l, 3])
        sent(H.at[l, pl.ds(0, 28)], send.at[l, 4])
        sent(MX.at[l, pl.ds(0, 7)], send.at[l, 5])
        for kind in range(2):
            sent(SS.at[l, kind, pl.ds(0, 7)], send.at[l, 6 + kind])

        @pl.when(s < NSEQ - 2)
        def _():
            sent(KV.at[l, 1], send.at[l, 8])

        @pl.when((y == 0) & (s < NSEQ - 8))
        def _():
            sent(RB.at[l], send.at[l, 11])

        @pl.when((core == 0) | (s >= 2))
        def _():
            sent(KV.at[l, 2], send.at[l, 9])

        @pl.when(((core == 0) & (s >= 2)) | ((core == 1) & (s < NSEQ - 3)))
        def _():
            sent(KV.at[l, 0, :, :, late], send.at[l, 10])


def row_factors(scale_codes, first_row, rows):
    blocks = (first_row + jnp.arange(rows, dtype=jnp.int32)) // BLOCK
    pick = blocks[:, None] == jnp.arange(scale_codes.shape[1], dtype=jnp.int32)[None, :]
    factor = jnp.exp2(scale_codes.astype(F32) - 127.0)
    return jnp.sum(jnp.where(pick[None, :, :, None], factor[:, None], 0.0), axis=2)


def per_device(
    hidden,
    q_weight,
    k_weight,
    v_weight,
    o_weight,
    q_scale,
    k_scale,
    v_scale,
    o_scale,
    in_gain,
    post_gain,
    q_gain,
    k_gain,
    windows,
):
    s = lax.axis_index("seq")
    w = lax.axis_index("wgt")
    scales = jnp.concatenate([q_scale, k_scale, v_scale], axis=2)
    factors = jnp.repeat(row_factors(scales, ROWS * s, ROWS), BLOCK, axis=2).astype(BF)
    wa = q_weight * factors[:, :, :256]
    wb = jnp.concatenate([k_weight, v_weight], axis=2) * factors[:, :, 256:]
    o_rows = jnp.exp2(
        lax.dynamic_slice_in_dim(o_scale, s // 2, 1, axis=1).astype(F32) - 127.0
    )
    columns = (w * WIDTH + jnp.arange(WIDTH, dtype=jnp.int32)) // BLOCK
    pick = columns[:, None] == jnp.arange(D // BLOCK, dtype=jnp.int32)[None, :]
    o_factor = jnp.sum(jnp.where(pick[None], o_rows, 0.0), axis=2).astype(BF)
    wo = (o_weight * o_factor[:, None, :]).reshape(LAYERS, 2, 32, WIDTH)
    gin = lax.dynamic_slice_in_dim(in_gain, w * WIDTH, WIDTH, axis=1)
    gains = jnp.concatenate(
        [
            jnp.concatenate([gin, post_gain, jnp.zeros((4, WIDTH), F32)], axis=0),
            jnp.concatenate([q_gain, k_gain, jnp.zeros((4, HD), F32)], axis=0),
        ],
        axis=1,
    ).T
    half = HD // 2
    position = s * TOK + jnp.arange(TOK, dtype=jnp.int32)
    inverse = rope_base ** (-jnp.arange(half, dtype=F32) * 2.0 / HD)
    angles = inverse[:, None] * position.astype(F32)[None, :]
    hid = hidden.T.reshape(4, ROWS, TOK)

    vmem = pl.BlockSpec(memory_space=pltpu.VMEM)
    dma = pltpu.SemaphoreType.DMA
    state = pl.pallas_call(
        kernel,
        out_shape=jax.ShapeDtypeStruct((4, ROWS, TOK), BF),
        in_specs=[vmem] * 7 + [pl.BlockSpec(memory_space=pltpu.SMEM)],
        out_specs=vmem,
        scratch_shapes=[
            pltpu.VMEM((LAYERS, 32, ROWS, TOK), BF),
            pltpu.VMEM((LAYERS, NSEQ, ROWS, 256), BF),
            pltpu.VMEM((LAYERS, NSEQ, ROWS, 256), BF),
            pltpu.VMEM((LAYERS, 2 * NSEQ, 32, WIDTH), BF),
            pltpu.VMEM((LAYERS, NWGT, 4, HD // 2, TOK), BF),
            pltpu.VMEM((LAYERS, 4, 2, HD, TOK), BF),
            pltpu.VMEM((LAYERS, 2, NWGT, 1, TOK), F32),
            pltpu.VMEM((512, TOK), F32),
            pltpu.VMEM((2, HD, TOK), BF),
            pltpu.VMEM((1, TOK), F32),
            pltpu.VMEM((TOK, HD), BF),
            pltpu.VMEM((2, TOK, TOK), F32),
            pltpu.VMEM((2, TOK, TOK), BF),
            pltpu.VMEM((2, 1, TOK), F32),
            pltpu.VMEM((2, HD, TOK), F32),
            pltpu.VMEM((LAYERS, HD // 2, TOK), BF),
            pltpu.VMEM((WIDTH, TOK), F32),
            dma((LAYERS, 2, 4, 4)),
            dma((LAYERS, 2, 4, 4)),
            dma((LAYERS, 4, 2, 4)),
            dma((LAYERS, 4, 2, 4)),
            dma((LAYERS, 4, 2)),
            dma((LAYERS, 4)),
            dma((LAYERS, 2)),
            dma((LAYERS, 12)),
        ],
        compiler_params=pltpu.CompilerParams(
            collective_id=0, has_side_effects=True, vmem_limit_bytes=44 * 1024 * 1024
        ),
    )(
        hid,
        wa,
        wb,
        wo,
        gains,
        jnp.cos(angles),
        jnp.sin(angles),
        windows,
    )
    return state.reshape(WIDTH, TOK).T


def solution(mesh):
    in_specs = (
        P("seq", "wgt"),
        P(None, "seq", "wgt"),
        P(None, "seq", "wgt"),
        P(None, "seq", "wgt"),
        P(None, "seq", "wgt"),
        P(None, None, "wgt"),
        P(None, None, "wgt"),
        P(None, None, "wgt"),
        P(),
        P(),
        P(None, "wgt"),
        P(),
        P(),
        P(),
    )
    return jax.shard_map(
        per_device, mesh=mesh, in_specs=in_specs, out_specs=P("seq", "wgt"), check_vma=False
    )
```

time: 202 us -> 158 us (0.78)
  the two profiles are of different devices: /device:TPU:64 before, /device:TPU:224 now
where the time goes in v3:
time: 158 us
  Pallas kernels  151 us (96%)
  local copies, waits for them, and re-layouts  4.95 us (3%)
  other arithmetic  1.85 us (1%)
    pallas_call x1, Pallas kernels, per_device(): pl.pallas_call(kernel, out_shape=jax.ShapeDtypeStruct((4, ROWS, TOK), BF)...  151 us
    unnamed x27, local copies, waits for them, and re-layouts  3.77 us

profile of v3, /device:TPU:224, one launch (start us, length us, event | category | flops | bytes accessed | tf_op | source)
XLA Modules:
  0.0 158.2 jit_solution(12909083193814558710)
XLA Ops:
  0.0 0.7 multiply_exponential_fusion
  0.8 0.0 copy-start.8
  0.8 0.0 copy-start.11
  0.8 0.0 copy-start.12
  0.8 0.6 copy-done.8
  1.4 0.0 copy-done.11
  1.5 0.0 copy-done.12
  1.5 0.1 constant_dynamic-slice_fusion
  1.6 0.0 copy-start.7
  1.6 0.0 copy-start.10
  1.7 0.6 copy-done.7
  2.3 0.0 copy-done.9
  2.3 0.1 maximum_maximum_fusion
  2.4 0.1 copy.24
  2.6 0.2 select_reduce_fusion.1
  2.8 0.1 copy.22
  2.9 0.2 select_reduce_fusion
  3.1 0.2 copy.23
  3.3 0.0 copy-done.3
  3.3 0.4 multiply_sine_fusion
  3.7 0.4 broadcast_in_dim.64
  4.1 0.0 copy-start.4
  4.2 0.0 copy-start.5
  4.2 0.1 convert_element_type.33
  4.3 0.7 copy-done.4
  5.1 0.1 copy-done.5
  5.1 0.0 copy-done.6
  5.2 0.1 slice_multiply_fusion
  5.3 0.2 copy.25
  5.5 0.7 copy-done.1
  6.2 151.2 %shard_map.136 = bf16[4,168,384]{2,1,0:T(8,128)(2,1)S(1)} custom-call(bf16[4,168,384]{2,1,0:T(8,128)(2,1)S(1)} %bitcast.12, bf16[2,168,256]{2,1,0:T(8,128)(2,1)S(1)} %get-tuple-element.6.wa, bf16[2,168,256]{2,1,0:T(8,128)(2,1)S(1)} %get-tuple-element.5.wb, bf16[2,2,32,672]{3,2,1,0:T(8,128)(2,1)S(1)} %bitcast.11, f32[800,8]{1,0:T(8,128)S(1)} %bitcast.10, ...), custom_call_target="tpu_custom_call" | custom-call | tf_op jit(solution)/shard_map/pallas_call | solution.py:686
  157.4 0.8 copy.27
  (19 shorter events, 0.1 us)
Async XLA Ops:
  0.0 1.5 copy-start
  0.8 0.7 copy-start.8
  0.8 0.7 copy-start.11
  0.8 0.7 copy-start.12
  1.6 0.7 copy-start.7
  1.6 0.7 copy-start.9
  1.6 0.7 copy-start.10
  2.3 0.9 copy-start.3
  4.1 0.9 copy-start.4
  4.2 1.0 copy-start.5
  4.2 1.0 copy-start.6
  5.2 1.0 copy-start.1
  5.5 0.8 copy-start.2

commit v4 on v3

--- a/solution.py
+++ b/solution.py
@@ -105,7 +105,7 @@
 
     tasks = {}
     for l in range(2):
-        tasks["scale", l] = (0.3, [("fin", l - 1)] if l else [], 0)
+        tasks["scale", l] = (0.3, [("fin", 0)] if l else [("wown", 0)], 0)
         tasks["wown", l] = (0.05, [("att0", 0)] if l else [], 1)
         tasks["oown", l] = (0.05, ([("scale", 1)] if l else []) + [("w", l, h, dz, 0) for h in (0, 1) for dz in (1, 2, 3)], 1)
         tasks["hz", l] = (0.05, [("scale", l)] + [("w", l, h, dz, 0) for h in (0, 1) for dz in (1, 3)], 0)
@@ -207,7 +207,7 @@
 
 
 def kernel(
-    hid, wa, wb, wo, gains, cosine, sine, windows,
+    hid, wq, wk, wv, wo, factors, o_factors, gains, cosine, sine, windows,
     out,
     H, WA, WB, O, MX, KV, SS, acc, Q, ROW, KX, SC, PB, TOT, MIX, RB, proj,
     w_recv, o_recv, h_recv, mx_recv, kv_recv, sib_recv, ss_recv, send,
@@ -333,14 +333,23 @@
     def gain(l, kind, rows):
         return gains[rows, 2 * kind + l : 2 * kind + l + 1]
 
+    def dequantize(l):
+        for j, (dst, src) in enumerate(
+            (
+                (WA.at[l, s, :, 0:128], wq.at[l, :, 0:128]),
+                (WA.at[l, s, :, 128:256], wq.at[l, :, 128:256]),
+                (WB.at[l, s, :, 0:128], wk.at[l]),
+                (WB.at[l, s, :, 128:256], wv.at[l]),
+            )
+        ):
+            dst[...] = src[...] * factors[l, :, j : j + 1]
+        for half in range(2):
+            O[l, 2 * s + half] = wo[l, 32 * half : 32 * half + 32] * o_factors[l : l + 1]
+
+    dequantize(0)
     for l in range(LAYERS):
-        WA[l, s] = wa[l]
-        WB[l, s] = wb[l]
-        for half in range(2):
-            O[l, 2 * s + half] = wo[l, half]
         for slot in range(3):
             KV[l, slot] = jnp.zeros((2, HD, TOK), BF)
-    out[...] = hid[...]
 
     barrier = pltpu.get_barrier_semaphore()
     neighbours = [here]
@@ -356,17 +365,23 @@
     late = pl.ds(128, 256)
 
     def scale(l):
+        row = lax.rsqrt(all_squares(l - 1, 1) / D + eps) if l else None
         squares = jnp.zeros((1, TOK), F32)
-        for i in range(4):
-            state = out[i].astype(F32)
+        for i in (0, 3, 1, 2):
+            if l == 0:
+                out[i] = hid[i]
+                state = hid[i].astype(F32)
+            else:
+                out[i] = next_state(l - 1, i, row)
+                state = out[i].astype(F32)
             H[l, 4 * w + i] = (state * gain(l, 0, pl.ds(ROWS * i, ROWS))).astype(BF)
             squares += jnp.sum(state * state, axis=0, keepdims=True)
-        for i in range(4):
+            h_to(l, i, (0, 0), (1, 0) if i < 2 else (3, 0))
+        for i in (2, 3):
             h_to(l, i, (0, 0), (1, 0))
             h_to(l, 3 - i, (0, 0), (3, 0))
         share_squares(l, 0, squares)
         acc[...] = jnp.zeros_like(acc)
-
     def multiply(l, half, first, last):
         buf, rows = ((WA, pl.ds(0, 256)), (WB, pl.ds(256, 256)))[half]
 
@@ -548,11 +563,16 @@
             squares += jnp.sum(part * part, axis=0, keepdims=True)
         share_squares(l, 1, squares)
 
+    def next_state(l, i, row):
+        rows = pl.ds(ROWS * i, ROWS)
+        post = proj[rows] * row * gain(l, 1, rows)
+        return (out[i].astype(F32) + post).astype(BF)
+
     def finish(l):
-        row = lax.rsqrt(all_squares(l, 1) / D + eps)
-        for i in range(4):
-            post = proj[ROWS * i : ROWS * (i + 1)] * row * gain(l, 1, pl.ds(ROWS * i, ROWS))
-            out[i] = (out[i].astype(F32) + post).astype(BF)
+        if l == LAYERS - 1:
+            row = lax.rsqrt(all_squares(l, 1) / D + eps)
+            for i in range(4):
+                out[i] = next_state(l, i, row)
 
     steps = []
     for name in schedule():
@@ -585,6 +605,8 @@
         elif kind == "hz":
             for i in (0, 3, 1, 2):
                 h_to(l, i, (0, 0), (0, 1))
+            if l == 0:
+                dequantize(1)
         elif kind == "wsib":
             half = which[0]
             arrived((WA, WB)[half].at[l, pl.ds(0, 16)], sib_recv.at[l, half])
@@ -657,16 +679,13 @@
     s = lax.axis_index("seq")
     w = lax.axis_index("wgt")
     scales = jnp.concatenate([q_scale, k_scale, v_scale], axis=2)
-    factors = jnp.repeat(row_factors(scales, ROWS * s, ROWS), BLOCK, axis=2).astype(BF)
-    wa = q_weight * factors[:, :, :256]
-    wb = jnp.concatenate([k_weight, v_weight], axis=2) * factors[:, :, 256:]
+    factors = row_factors(scales, ROWS * s, ROWS).astype(BF)
     o_rows = jnp.exp2(
         lax.dynamic_slice_in_dim(o_scale, s // 2, 1, axis=1).astype(F32) - 127.0
     )
     columns = (w * WIDTH + jnp.arange(WIDTH, dtype=jnp.int32)) // BLOCK
     pick = columns[:, None] == jnp.arange(D // BLOCK, dtype=jnp.int32)[None, :]
     o_factor = jnp.sum(jnp.where(pick[None], o_rows, 0.0), axis=2).astype(BF)
-    wo = (o_weight * o_factor[:, None, :]).reshape(LAYERS, 2, 32, WIDTH)
     gin = lax.dynamic_slice_in_dim(in_gain, w * WIDTH, WIDTH, axis=1)
     gains = jnp.concatenate(
         [
@@ -686,7 +705,7 @@
     state = pl.pallas_call(
         kernel,
         out_shape=jax.ShapeDtypeStruct((4, ROWS, TOK), BF),
-        in_specs=[vmem] * 7 + [pl.BlockSpec(memory_space=pltpu.SMEM)],
+        in_specs=[vmem] * 10 + [pl.BlockSpec(memory_space=pltpu.SMEM)],
         out_specs=vmem,
         scratch_shapes=[
             pltpu.VMEM((LAYERS, 32, ROWS, TOK), BF),
@@ -720,9 +739,12 @@
         ),
     )(
         hid,
-        wa,
-        wb,
-        wo,
+        q_weight,
+        k_weight,
+        v_weight,
+        o_weight,
+        factors,
+        o_factor,
         gains,
         jnp.cos(angles),
         jnp.sin(angles),

time: 158 us -> 154 us (0.975)
  the two profiles are of different devices: /device:TPU:224 before, /device:TPU:64 now
where the time goes in v4:
time: 154 us; the launch traced here: 153 us
  Pallas kernels  148 us (96%)
  local copies, waits for them, and re-layouts  3.49 us (2%)
  other arithmetic  1.72 us (1%)
    pallas_call x1, Pallas kernels, per_device(): pl.pallas_call(kernel, out_shape=jax.ShapeDtypeStruct((4, ROWS, TOK), BF)...  148 us

profile of v4, /device:TPU:64, one launch (start us, length us, event | category | flops | bytes accessed | tf_op | source)
XLA Modules:
  0.0 153.4 jit_solution(16855898872965691332)
XLA Ops:
  0.0 0.0 copy-start
  0.0 0.7 multiply_exponential_fusion
  0.8 0.0 copy-start.8
  0.8 0.0 copy-start.11
  0.8 0.0 copy-start.12
  0.8 0.6 copy-done.8
  1.4 0.0 copy-done.11
  1.5 0.0 copy-done.12
  1.5 0.0 copy-start.7
  1.5 0.0 copy-start.9
  1.5 0.0 copy-start.10
  1.5 0.1 constant_dynamic-slice_fusion
  1.7 0.5 copy-done.7
  2.2 0.0 copy-done.9
  2.2 0.0 copy-done.10
  2.2 0.1 maximum_maximum_fusion
  2.3 0.1 copy.27
  2.4 0.2 select_reduce_fusion.1.o_factors
  2.7 0.1 copy.26
  2.8 0.2 select_reduce_fusion
  3.0 0.2 copy.29.factors
  3.1 0.0 copy-start.4
  3.2 0.4 multiply_sine_fusion
  3.6 0.0 copy-start.2
  3.6 0.0 copy-start.3
  3.6 0.2 copy.28
  3.8 0.0 copy-start.6
  3.8 0.3 copy-done.4
  4.1 0.5 copy-done.2
  4.5 0.1 copy-done.3
  4.6 148.0 %shard_map.136 = bf16[4,168,384]{2,1,0:T(8,128)(2,1)S(1)} custom-call(bf16[4,168,384]{2,1,0:T(8,128)(2,1)S(1)} %bitcast.10, bf16[2,168,256]{2,1,0:T(8,128)(2,1)S(1)} %copy-done.3, bf16[2,168,128]{2,1,0:T(8,128)(2,1)S(1)} %copy-done.4, bf16[2,168,128]{2,1,0:T(8,128)(2,1)S(1)} %copy-done.5, bf16[2,64,672]{2,1,0:T(8,128)(2,1)S(1)} %copy-done.2, ...), custom_call_target="tpu_custom_call" | custom-call | tf_op jit(solution)/shard_map/pallas_call | solution.py:705
  152.6 0.8 copy.31
  (15 shorter events, 0.1 us)
Async XLA Ops:
  0.0 1.5 copy-start
  0.8 0.7 copy-start.8
  0.8 0.7 copy-start.11
  0.8 0.7 copy-start.12
  1.5 0.7 copy-start.7
  1.5 0.7 copy-start.9
  1.5 0.7 copy-start.10
  1.6 2.2 %copy-start.5 = (bf16[2,168,128]{2,1,0:T(8,128)(2,1)S(1)}, bf16[2,168,128]{2,1,0:T(8,128)(2,1)}, u32[]{:S(2)}) copy-start(bf16[2,168,128]{2,1,0:T(8,128)(2,1)} %wv.1) | copy-start | bytes 258052
  2.2 1.6 %copy-start.1 = (bf16[384,672]{0,1:T(8,128)(2,1)S(1)}, bf16[384,672]{0,1:T(8,128)(2,1)}, u32[]{:S(2)}) copy-start(bf16[384,672]{0,1:T(8,128)(2,1)} %param.14) | copy-start | bytes 1548292
  3.1 0.9 copy-start.4
  3.6 0.9 copy-start.2
  3.6 1.0 copy-start.3
  3.8 0.8 copy-start.6

commit v5 on v4

--- a/solution.py
+++ b/solution.py
@@ -69,7 +69,7 @@
 BY_Z = {"h": H_BY_Z, "m": M_BY_Z}
 
 
-SLACK = ((0.5, 1.0), (4.0, 4.0))
+SLACK = ((0.5, 3.0), (6.0, 5.0))
 
 
 def schedule():
@@ -181,7 +181,8 @@
     def eff(ev):
         t = arrival[ev]
         if ev[0] == "w":
-            return t + SLACK[ev[1]][ev[2] // 2]
+            slack = SLACK[ev[1]][ev[2] // 2]
+            return t + (min(slack, 4.0) if ("scale", 1) in done else slack)
         if ev[0] in "hm" and ev[3:] == (0, 1):
             return t + 0.5
         return t

time: 154 us -> 153 us (level); the launches traced: 153 us -> 150 us
  Pallas kernels: 148 us -> 145 us
    pallas_call x1, Pallas kernels: 148 us -> 145 us  [per_device(): pl.pallas_call(kernel, out_shape=jax.ShapeDtypeStruct((4, ROWS, TOK), BF)...]
where the time goes in v5:
time: 153 us; the launch traced here: 150 us
  Pallas kernels  145 us (95%)
  local copies, waits for them, and re-layouts  3.49 us (2%)
  other arithmetic  1.72 us (1%)
    pallas_call x1, Pallas kernels, per_device(): pl.pallas_call(kernel, out_shape=jax.ShapeDtypeStruct((4, ROWS, TOK), BF)...  145 us

profile of v5, /device:TPU:64, one launch (start us, length us, event | category | flops | bytes accessed | tf_op | source)
XLA Modules:
  0.0 149.9 jit_solution(8648091475256596347)
XLA Ops:
  0.0 0.0 copy-start
  0.0 0.7 multiply_exponential_fusion
  0.8 0.0 copy-start.8
  0.8 0.0 copy-start.11
  0.8 0.0 copy-start.12
  0.8 0.6 copy-done.8
  1.4 0.0 copy-done.11
  1.5 0.0 copy-done.12
  1.5 0.0 copy-done
  1.5 0.0 copy-start.7
  1.5 0.0 copy-start.9
  1.5 0.0 copy-start.10
  1.5 0.1 constant_dynamic-slice_fusion
  1.7 0.5 copy-done.7
  2.2 0.0 copy-done.9
  2.2 0.1 maximum_maximum_fusion
  2.3 0.1 copy.27
  2.4 0.2 select_reduce_fusion.1.o_factors
  2.7 0.1 copy.26
  2.8 0.2 select_reduce_fusion
  3.0 0.2 copy.29.factors
  3.1 0.0 copy-start.4
  3.2 0.4 multiply_sine_fusion
  3.6 0.0 copy-start.2
  3.6 0.0 copy-start.3
  3.6 0.2 copy.28
  3.8 0.0 copy-start.6
  3.8 0.3 copy-done.4
  4.1 0.5 copy-done.2
  4.5 0.1 copy-done.3
  4.6 144.5 %shard_map.136 = bf16[4,168,384]{2,1,0:T(8,128)(2,1)S(1)} custom-call(bf16[4,168,384]{2,1,0:T(8,128)(2,1)S(1)} %bitcast.10, bf16[2,168,256]{2,1,0:T(8,128)(2,1)S(1)} %copy-done.3, bf16[2,168,128]{2,1,0:T(8,128)(2,1)S(1)} %copy-done.4, bf16[2,168,128]{2,1,0:T(8,128)(2,1)S(1)} %copy-done.5, bf16[2,64,672]{2,1,0:T(8,128)(2,1)S(1)} %copy-done.2, ...), custom_call_target="tpu_custom_call" | custom-call | tf_op jit(solution)/shard_map/pallas_call | solution.py:706
  149.1 0.8 copy.31
  (15 shorter events, 0.1 us)
Async XLA Ops:
  0.0 1.5 copy-start
  0.8 0.7 copy-start.8
  0.8 0.7 copy-start.11
  0.8 0.7 copy-start.12
  1.5 0.7 copy-start.7
  1.5 0.7 copy-start.9
  1.5 0.7 copy-start.10
  1.6 2.2 %copy-start.5 = (bf16[2,168,128]{2,1,0:T(8,128)(2,1)S(1)}, bf16[2,168,128]{2,1,0:T(8,128)(2,1)}, u32[]{:S(2)}) copy-start(bf16[2,168,128]{2,1,0:T(8,128)(2,1)} %wv.1) | copy-start | bytes 258052
  2.2 1.6 %copy-start.1 = (bf16[384,672]{0,1:T(8,128)(2,1)S(1)}, bf16[384,672]{0,1:T(8,128)(2,1)}, u32[]{:S(2)}) copy-start(bf16[384,672]{0,1:T(8,128)(2,1)} %param.14) | copy-start | bytes 1548292
  3.1 0.9 copy-start.4
  3.6 0.9 copy-start.2
  3.6 1.0 copy-start.3
  3.8 0.8 copy-start.6
